TPU v7x, 512 devices: a 4x2x32 block of a 4x8x32 slice. The times are simulated.
512 devices in a mesh: groups: 2 (over y), ep: 32 (over z), tp: 4 (over x), dp: 2 (over core).
Axes of the slice: x: 4, y: 2, z: 32, core: 2. Of those that a mesh axis runs over, the one named last changes fastest.
The devices are a block of a 4x8x32 slice.
Arguments:
- tokens: bfloat16 [8192, 1536], P(('groups', 'ep', 'tp', 'dp')), parts along dimension 0, may hold values from -6 to 6
- expert_ids: int32 [8192, 4], P(('groups', 'ep', 'tp', 'dp')), parts along dimension 0, may hold values from 0 to 63, all different within a row; in each aligned block of 16 rows (0 to 15, 16 to 31, ...) at most 2 rows name the same one
- gate_weights: float32 [8192, 4], P(('groups', 'ep', 'tp', 'dp')), parts along dimension 0, may hold values from 0.1 to 1
- w_gate: bfloat16 [64, 1536, 1536], P(('ep', 'dp'), None, 'tp'), may hold values from -0.15625 to 0.15625
- w_up: bfloat16 [64, 1536, 1536], P(('ep', 'dp'), None, 'tp'), may hold values from -0.15625 to 0.15625
- w_down: bfloat16 [64, 1536, 1536], P(('ep', 'dp'), None, 'tp'), may hold values from -0.15625 to 0.15625
Outputs:
- mixed: bfloat16 [8192, 1536], P(('groups', 'ep', 'tp', 'dp')), parts along dimension 0
- expert_loads: int32 [128], P('groups'), parts along dimension 0
There are 2 independent parts, one for each index of `groups`. A program takes and returns all parts, laid end to end along the dimension named above; an argument that names none is the same for every part. Nothing has to cross between parts.
Inputs may be any that keep to these rules, and one draw needn't show every extreme that they name: `expert_ids`: each row names 4 different experts. In each aligned block of 16 rows (the rows of one device) no expert is named by more than 2 rows, and in some blocks one expert is named by exactly 2 rows.
All inputs are finite; a program needn't handle non-finite values.
Results may differ from a plain program's by a relative error of at most 0.0057.
Values may be sent and summed in bfloat16 or wider, within the bound.
No kernel may reach another device: no remote copies, remote signals or barrier semaphores. Data moves between devices by JAX's collectives and lax.ppermute only.
A program may use at most 64 MiB of HBM per device.

v0:
```python
import jax
import jax.numpy as jnp
from jax import lax
from jax.sharding import PartitionSpec as P


def one_axis_at_a_time(array, axes):
    for axis in axes:
        array = lax.psum(array, axis)
    return array


def copy_for_each(array, axis):
    copies = jnp.broadcast_to(array, (lax.axis_size(axis), *array.shape))
    return lax.all_to_all(copies, axis, split_axis=0, concat_axis=0, tiled=True)


def laid_out(blocks, dim):
    shape = list(blocks.shape[1:])
    shape[dim] *= blocks.shape[0]
    return jnp.moveaxis(blocks, 0, dim).reshape(shape)


def collect(array, axis, dim):
    blocks = copy_for_each(array, axis)
    return laid_out(blocks, dim)


def split_up(array, dim, size):
    before, after = (array.shape[:dim], array.shape[dim + 1 :])
    return jnp.moveaxis(array.reshape(*before, size, -1, *after), dim, 0)


def sent_and_summed(array, axis, dim):
    blocks = split_up(array, dim, lax.axis_size(axis))
    arrived = lax.all_to_all(blocks, axis, split_axis=0, concat_axis=0, tiled=True)
    return arrived.sum(axis=0)


def expert_apply(token_rows, gate_part, up_part, down_part):
    gate_value = jnp.dot(token_rows, gate_part, preferred_element_type=jnp.float32)
    up_value = jnp.dot(token_rows, up_part, preferred_element_type=jnp.float32)
    hidden = (jax.nn.silu(gate_value) * up_value).astype(jnp.bfloat16)
    return lax.dot_general(
        hidden, down_part, (((1,), (1,)), ((), ())), preferred_element_type=jnp.float32
    )


def per_device(tokens, expert_ids, gate_weights, w_gate, w_up, w_down):
    tok_rows = tokens.shape[0]
    model_width = tokens.shape[1]
    top_count = expert_ids.shape[1]
    ep_count = lax.axis_size("ep")
    dp_count = lax.axis_size("dp")
    experts = ep_count * dp_count
    capacity = max(2, 2 * tok_rows * top_count // experts)
    pair_ids = expert_ids.reshape(-1)
    expert_range = jnp.arange(experts, dtype=jnp.int32)
    onehot = (pair_ids[:, None] == expert_range[None, :]).astype(jnp.int32)
    local_counts = jnp.sum(onehot, axis=0).astype(jnp.float32)
    expert_loads = one_axis_at_a_time(local_counts, ("ep", "tp", "dp")).astype(jnp.int32)
    earlier = (jnp.cumsum(onehot, axis=0) - onehot) * onehot
    slot_ranks = jnp.sum(earlier, axis=1)
    targets = pair_ids * capacity + slot_ranks
    slot_range = jnp.arange(experts * capacity, dtype=jnp.int32)
    selector = jnp.any(
        targets.reshape(tok_rows, top_count)[None, :, :] == slot_range[:, None, None], axis=2
    )
    outgoing = jnp.dot(selector.astype(jnp.bfloat16), tokens, preferred_element_type=jnp.float32)
    outgoing = outgoing.astype(jnp.bfloat16).reshape(experts, capacity, model_width)
    arrived = lax.all_to_all(outgoing, ("ep", "dp"), split_axis=0, concat_axis=0, tiled=True)
    gate_local = w_gate[0]
    up_local = w_up[0]
    down_local = w_down[0]
    fragment = collect(arrived, "tp", 0)
    flat_rows = fragment.reshape(-1, model_width)
    partial_value = expert_apply(flat_rows, gate_local, up_local, down_local)
    partial_terms = partial_value.reshape(fragment.shape[0], capacity, model_width)
    finished = sent_and_summed(partial_terms, "tp", 0).astype(jnp.bfloat16)
    returned = lax.all_to_all(finished, ("ep", "dp"), split_axis=0, concat_axis=0, tiled=True)
    returned = returned.reshape(experts * capacity, model_width)
    picked = jnp.take(returned, targets, axis=0).reshape(tok_rows, top_count, model_width)
    mixed = jnp.sum(gate_weights[:, :, None] * picked.astype(jnp.float32), axis=1)
    return (mixed.astype(jnp.bfloat16), expert_loads)


def solution(mesh):
    return jax.shard_map(
        per_device,
        mesh=mesh,
        in_specs=(
            P(("groups", "ep", "tp", "dp"), None),
            P(("groups", "ep", "tp", "dp"), None),
            P(("groups", "ep", "tp", "dp"), None),
            P(("ep", "dp"), None, "tp"),
            P(("ep", "dp"), None, "tp"),
            P(("ep", "dp"), None, "tp"),
        ),
        out_specs=(P(("groups", "ep", "tp", "dp"), None), P("groups")),
        check_vma=False,
    )
```

profile of v0, /device:TPU:40, one launch (start us, length us, event | category | flops | bytes accessed | tf_op | source)
XLA Modules:
  0.0 284.0 jit_solution(17129399234200269265)
XLA Ops:
  0.6 0.0 copy-start
  0.6 0.9 copy.27
  1.5 0.1 reshape.64
  1.6 0.1 fusion.7
  1.7 0.1 reduce_window_sum.11
  1.8 0.2 fusion.9
  1.9 0.1 reduce_sum.41
  2.1 0.1 copy.29
  2.1 0.1 fusion.8
  2.2 1.1 convolution_convert_fusion
  3.3 0.1 reshape.65
  3.5 100.1 %all_to_all.20 = bf16[64,2,1536]{2,1,0:T(2,128)(2,1)S(1)} all-to-all(bf16[64,2,1536]{2,1,0:T(2,128)(2,1)S(1)} %reshape.65), channel_id=1, replica_groups=mesh['groups'=2,'ep'=32,'tp'=4,'dp'=2] {'ep','dp'}, dimensions={0} | all-to-all | bytes 786432 | tf_op jit(solution)/shard_map/all_to_all | solution.py:71
  103.6 0.8 broadcast_in_dim.17
  104.4 24.0 %all_to_all.21 = bf16[4,64,2,1536]{3,2,1,0:T(2,128)(2,1)S(1)} all-to-all(bf16[4,64,2,1536]{3,2,1,0:T(2,128)(2,1)S(1)} %broadcast_in_dim.17), channel_id=1, replica_groups=mesh['groups'=2,'ep'=32,'tp'=4,'dp'=2] {'tp'}, dimensions={0} | all-to-all | bytes 3145728 | tf_op jit(solution)/shard_map/all_to_all | solution.py:15
  128.4 1.5 reshape_reshape.4
  129.9 0.0 copy-start.1
  129.9 0.0 copy-start.3
  129.9 2.9 %fusion.4 = f32[512,384]{1,0:T(8,128)S(1)} fusion(bf16[512,1536]{1,0:T(8,128)(2,1)} %reshape_reshape.4, bf16[1,1536,384]{2,1,0:T(8,128)(2,1)} %param.9), kind=kOutput, calls=%fused_computation.7 | convolution fusion | flops 603979776 | bytes 3538944 | tf_op jit(solution)/shard_map/dot_general | solution.py:41
  132.8 0.0 copy-done.1
  132.8 0.0 copy-done.3
  132.8 1.0 fusion
  133.8 0.1 dot_general.17
  134.0 0.0 copy-done
  134.0 1.0 fusion.1
  135.0 38.7 %all_to_all.22 = f32[4,64,2,1536]{3,1,2,0:T(8,128)} all-to-all(f32[4,64,2,1536]{3,1,2,0:T(8,128)S(1)} %fusion.1), channel_id=1, replica_groups=mesh['groups'=2,'ep'=32,'tp'=4,'dp'=2] {'tp'}, dimensions={0} | all-to-all | bytes 6291456 | tf_op jit(solution)/shard_map/all_to_all | solution.py:36
  173.7 2.2 reduce_sum.42
  175.9 0.0 copy-start.2
  175.9 1.1 copy.31
  177.0 7.5 %all-to-all-start.3 = ((bf16[64,2,1536]{2,1,0:T(2,128)(2,1)}), bf16[64,2,1536]{2,1,0:T(2,128)(2,1)S(1)}, u32[]{:S(2)}, u32[]{:S(2)}) async-start(bf16[64,2,1536]{2,1,0:T(2,128)(2,1)} %copy.31), calls=%async_computation.3 | async-start | bytes 786432 | tf_op jit(solution)/shard_map/all_to_all | solution.py:80
  184.6 0.1 mul.45
  184.7 0.0 copy-done.2
  184.7 0.1 copy.26
  184.8 85.2 %psum.21 = f32[64]{0:T(128)S(1)} all-reduce(f32[64]{0:T(128)S(1)} %convert_element_type.31), channel_id=1, replica_groups=mesh['groups'=2,'ep'=32,'tp'=4,'dp'=2] {'ep'}, use_global_device_ids=true, to_apply=%region_6.7 | all-reduce | flops 64 | bytes 512 | tf_op jit(solution)/shard_map/psum | solution.py:9
  270.0 8.9 %psum.22 = f32[64]{0:T(128)S(1)} all-reduce(f32[64]{0:T(128)S(1)} %psum.21), channel_id=1, replica_groups=mesh['groups'=2,'ep'=32,'tp'=4,'dp'=2] {'tp'}, use_global_device_ids=true, to_apply=%region_7.8 | all-reduce | flops 64 | bytes 512 | tf_op jit(solution)/shard_map/psum | solution.py:9
  278.9 2.5 psum.23
  281.4 0.5 convert_element_type.32
  282.0 0.0 all-to-all-done.3
  282.0 0.1 reshape.66
  282.1 0.7 gather_fusion
  282.9 0.1 gather.7
  282.9 1.1 multiply_reduce_fusion
  (5 shorter events, 0.0 us)
Async XLA Ops:
  0.6 133.3 %copy-start = (bf16[1,1536,384]{2,1,0:T(8,128)(2,1)S(1)}, bf16[1,1536,384]{2,1,0:T(8,128)(2,1)}, u32[]{:S(2)}) copy-start(bf16[1,1536,384]{2,1,0:T(8,128)(2,1)} %param.11) | copy-start | bytes 3538948
  129.9 2.9 %copy-start.1 = (bf16[512,1536]{1,0:T(8,128)(2,1)S(1)}, bf16[512,1536]{1,0:T(8,128)(2,1)}, u32[]{:S(2)}) copy-start(bf16[512,1536]{1,0:T(8,128)(2,1)} %reshape_reshape.4) | copy-start | bytes 4718596
  129.9 2.9 %copy-start.3 = (bf16[1,1536,384]{2,1,0:T(8,128)(2,1)S(1)}, bf16[1,1536,384]{2,1,0:T(8,128)(2,1)}, u32[]{:S(2)}) copy-start(bf16[1,1536,384]{2,1,0:T(8,128)(2,1)} %param.10) | copy-start | bytes 3538948
  175.9 8.8 %copy-start.2 = (f32[16,4]{0,1:T(4,128)S(1)}, f32[16,4]{0,1:T(4,128)}, u32[]{:S(2)}) copy-start(f32[16,4]{0,1:T(4,128)} %param.8) | copy-start | bytes 772
  177.0 104.9 %all-to-all-start.3 = ((bf16[64,2,1536]{2,1,0:T(2,128)(2,1)}), bf16[64,2,1536]{2,1,0:T(2,128)(2,1)S(1)}, u32[]{:S(2)}, u32[]{:S(2)}) async-start(bf16[64,2,1536]{2,1,0:T(2,128)(2,1)} %copy.31), calls=%async_computation.3 | async-start | bytes 786432 | tf_op jit(solution)/shard_map/all_to_all | solution.py:80
where the time goes:
time: 286 us; the launch traced here: 284 us
  blocking collectives  259 us (91%)
  starting transfers between devices  7.55 us (3%)
  matrix products  5.98 us (2%)
  local copies, waits for them, and re-layouts  5.97 us (2%)
  other arithmetic  4.29 us (2%)
    all_to_all x1, blocking collectives, per_device(): lax.all_to_all(outgoing, ('ep', 'dp'), split_axis=0, concat_axis=0, tiled...  100 us
    psum x3, blocking collectives, one_axis_at_a_time(): array = lax.psum(array, axis)  96.6 us
    all_to_all x1, blocking collectives, sent_and_summed(): lax.all_to_all(blocks, axis, split_axis=0, concat_axis=0, tiled=True)  38.7 us
    all_to_all x1, blocking collectives, copy_for_each(): return lax.all_to_all(copies, axis, split_axis=0, concat_axis=0, tiled=True)  24 us
    all_to_all x1, starting transfers between devices, per_device(): lax.all_to_all(finished, ('ep', 'dp'), split_axis=0, concat_axis=0, tiled...  7.55 us
  transfers between devices with their start and end apart: 1, of which 0 were waited for; matrix products, arithmetic and copies ran while one was open for 0% of the time, Pallas kernels for 0%

commit v1 on v0

v1 whole, which is shorter than its diff:
```python
import jax
import jax.numpy as jnp
from jax import lax
from jax.sharding import PartitionSpec as P

EMPTY = 8.0
DIGIT = 64


def copy_for_each(array, axis):
    copies = jnp.broadcast_to(array, (lax.axis_size(axis), *array.shape))
    return lax.all_to_all(copies, axis, split_axis=0, concat_axis=0, tiled=True)


def expert_apply(token_rows, gate_part, up_part, down_part):
    gate_value = jnp.dot(token_rows, gate_part, preferred_element_type=jnp.float32)
    up_value = jnp.dot(token_rows, up_part, preferred_element_type=jnp.float32)
    hidden = (jax.nn.silu(gate_value) * up_value).astype(jnp.bfloat16)
    return lax.dot_general(
        hidden, down_part, (((1,), (1,)), ((), ())), preferred_element_type=jnp.float32
    )


def per_device(tokens, expert_ids, gate_weights, w_gate, w_up, w_down):
    tok_rows, model_width = tokens.shape
    top_count = expert_ids.shape[1]
    experts = lax.axis_size("ep") * lax.axis_size("dp")
    capacity = max(2, 2 * tok_rows * top_count // experts)
    pair_ids = expert_ids.reshape(-1)
    expert_range = jnp.arange(experts, dtype=jnp.int32)
    onehot = (pair_ids[:, None] == expert_range[None, :]).astype(jnp.int32)
    earlier = (jnp.cumsum(onehot, axis=0) - onehot) * onehot
    slot_ranks = jnp.sum(earlier, axis=1)
    targets = pair_ids * capacity + slot_ranks
    slot_range = jnp.arange(experts * capacity, dtype=jnp.int32)
    selector = jnp.any(
        targets.reshape(tok_rows, top_count)[None, :, :] == slot_range[:, None, None], axis=2
    )
    empty = ~jnp.any(selector, axis=1)
    outgoing = jnp.dot(selector.astype(jnp.bfloat16), tokens, preferred_element_type=jnp.float32)
    first = jnp.arange(model_width, dtype=jnp.int32) == 0
    outgoing = jnp.where(empty[:, None] & first[None, :], EMPTY, outgoing)
    outgoing = outgoing.astype(jnp.bfloat16).reshape(experts, capacity, model_width)
    arrived = lax.all_to_all(outgoing, ("ep", "dp"), split_axis=0, concat_axis=0, tiled=True)
    fragment = copy_for_each(arrived, "tp")
    load = jnp.sum((fragment[..., 0] < EMPTY - 1).astype(jnp.int32))
    partial_value = expert_apply(
        fragment.reshape(-1, model_width), w_gate[0], w_up[0], w_down[0]
    ).astype(jnp.bfloat16)
    partial_terms = partial_value.reshape(fragment.shape)
    terms = lax.all_to_all(partial_terms, "tp", split_axis=0, concat_axis=0, tiled=True)
    finished = jnp.sum(terms.astype(jnp.float32), axis=0).astype(jnp.bfloat16)
    digits = jnp.where(jnp.arange(128) == 0, load // DIGIT, load % DIGIT).astype(jnp.bfloat16)
    finished = jnp.concatenate(
        [finished, jnp.broadcast_to(digits, (experts, capacity, 128))], axis=2
    )
    returned = lax.all_to_all(finished, ("ep", "dp"), split_axis=0, concat_axis=0, tiled=True)
    digits = returned[:, 0, model_width : model_width + 2].astype(jnp.int32)
    expert_loads = digits[:, 0] * DIGIT + digits[:, 1]
    returned = returned.reshape(experts * capacity, -1)
    picked = jnp.take(returned, targets, axis=0)[:, :model_width]
    picked = picked.reshape(tok_rows, top_count, model_width)
    mixed = jnp.sum(gate_weights[:, :, None] * picked.astype(jnp.float32), axis=1)
    return (mixed.astype(jnp.bfloat16), expert_loads)


def solution(mesh):
    return jax.shard_map(
        per_device,
        mesh=mesh,
        in_specs=(
            P(("groups", "ep", "tp", "dp"), None),
            P(("groups", "ep", "tp", "dp"), None),
            P(("groups", "ep", "tp", "dp"), None),
            P(("ep", "dp"), None, "tp"),
            P(("ep", "dp"), None, "tp"),
            P(("ep", "dp"), None, "tp"),
        ),
        out_specs=(P(("groups", "ep", "tp", "dp"), None), P("groups")),
        check_vma=False,
    )
```

time: 286 us -> 242 us (0.85)
  blocking collectives: 259 us -> 124 us
  waiting for transfers between devices: 0.01 us -> 70.4 us
  local copies, waits for them, and re-layouts: 5.97 us -> 14.8 us
  starting transfers between devices: 7.55 us -> 12.1 us
  matrix products: 5.98 us -> 9.61 us
  other arithmetic: 4.29 us -> 7.2 us
    psum x3 -> x0, blocking collectives: 96.6 us -> none  [one_axis_at_a_time(): array = lax.psum(array, axis)]
    all_to_all x1, waiting for transfers between devices: 0.01 us -> 55.5 us  [per_device(): lax.all_to_all(finished, ('ep', 'dp'), split_axis=0, concat_axis=0, tiled...]
    all_to_all x1 -> x0, blocking collectives: 38.7 us -> none  [sent_and_summed(): lax.all_to_all(blocks, axis, split_axis=0, concat_axis=0, tiled=True)]
    all_to_all x0 -> x1, waiting for transfers between devices: none -> 14.9 us  [per_device(): lax.all_to_all(partial_terms, 'tp', split_axis=0, concat_axis=0, tiled=True)]
    reshape x1 -> x3, local copies, waits for them, and re-layouts: 0.15 us -> 9.3 us  [the longest x1 4.64 us: per_device(): fragment.reshape(-1, model_width)]
    all_to_all x0 -> x1, starting transfers between devices: none -> 4.6 us  [per_device(): lax.all_to_all(partial_terms, 'tp', split_axis=0, concat_axis=0, tiled=True)]
    dot_general x1, matrix products: 1.02 us -> 4.9 us  [expert_apply(): lax.dot_general(hidden, down_part, (((1,), (1,)), ((), ())), preferred_el...]
  transfers between devices with their start and end apart: 1 -> 2, of which waited for: 0 -> 2; matrix products, arithmetic and copies ran while one was open for 0% -> 0% of each run, Pallas kernels for 0% -> 0%
where the time goes in v1:
time: 242 us
  blocking collectives  124 us (51%)
  waiting for transfers between devices  70.4 us (29%)
  local copies, waits for them, and re-layouts  14.8 us (6%)
  starting transfers between devices  12.1 us (5%)
  matrix products  9.61 us (4%)
  other arithmetic  7.2 us (3%)
  between operations  3.41 us (1%)
    all_to_all x1, blocking collectives, per_device(): lax.all_to_all(outgoing, ('ep', 'dp'), split_axis=0, concat_axis=0, tiled...  100 us
    all_to_all x1, waiting for transfers between devices, per_device(): lax.all_to_all(finished, ('ep', 'dp'), split_axis=0, concat_axis=0, tiled...  55.5 us
    all_to_all x1, blocking collectives, copy_for_each(): return lax.all_to_all(copies, axis, split_axis=0, concat_axis=0, tiled=True)  24 us
    all_to_all x1, waiting for transfers between devices, per_device(): lax.all_to_all(partial_terms, 'tp', split_axis=0, concat_axis=0, tiled=True)  14.9 us
    all_to_all x1, starting transfers between devices, per_device(): lax.all_to_all(finished, ('ep', 'dp'), split_axis=0, concat_axis=0, tiled...  7.55 us
    dot_general x1, matrix products, expert_apply(): lax.dot_general(hidden, down_part, (((1,), (1,)), ((), ())), preferred_el...  4.9 us
  transfers between devices with their start and end apart: 2, of which 2 were waited for; matrix products, arithmetic and copies ran while one was open for 0% of the time, Pallas kernels for 0%

profile of v1, /device:TPU:40, one launch (start us, length us, event | category | flops | bytes accessed | tf_op | source)
XLA Modules:
  0.0 241.6 jit_solution(13219548330450839437)
XLA Ops:
  0.6 0.0 copy-start
  0.7 0.9 copy.41
  1.5 0.1 reshape.80
  1.6 0.1 fusion.17
  1.7 0.1 reduce_window_sum.11
  1.8 0.2 select_reduce_fusion
  2.0 0.1 reduce_sum.44
  2.1 0.1 copy.43
  2.1 0.1 fusion.16
  2.3 1.1 fusion
  3.4 0.1 reshape.81
  3.5 100.1 %all_to_all.20 = bf16[64,2,1536]{2,1,0:T(2,128)(2,1)S(1)} all-to-all(bf16[64,2,1536]{2,1,0:T(2,128)(2,1)S(1)} %reshape.81), channel_id=1, replica_groups=mesh['groups'=2,'ep'=32,'tp'=4,'dp'=2] {'ep','dp'}, dimensions={0} | all-to-all | bytes 786432 | tf_op jit(solution)/shard_map/all_to_all | solution.py:44
  103.6 0.1 broadcast_in_dim.35
  103.8 24.0 %all_to_all.21 = bf16[4,64,2,1536]{3,1,2,0:T(8,128)(2,1)S(1)} all-to-all(bf16[4,64,2,1536]{3,1,2,0:T(8,128)(2,1)S(1)} %broadcast_in_dim.35), channel_id=1, replica_groups=mesh['groups'=2,'ep'=32,'tp'=4,'dp'=2] {'tp'}, dimensions={0} | all-to-all | bytes 3145728 | tf_op jit(solution)/shard_map/all_to_all | solution.py:12
  127.8 2.8 %copy.45 = bf16[4,64,2,1536]{3,2,1,0:T(2,128)(2,1)} copy(bf16[4,64,2,1536]{3,1,2,0:T(8,128)(2,1)S(1)} %all_to_all.21) | data formatting | bytes 3145728 | tf_op jit(solution)/shard_map/all_to_all | solution.py:12
  130.6 4.6 %reshape.82 = bf16[512,1536]{1,0:T(8,128)(2,1)} reshape(bf16[4,64,2,1536]{3,2,1,0:T(2,128)(2,1)} %copy.45) | data formatting | bytes 3145728 | tf_op jit(solution)/shard_map/reshape | solution.py:48
  135.2 3.6 %fusion.4 = f32[512,384]{1,0:T(8,128)} fusion(bf16[512,1536]{1,0:T(8,128)(2,1)} %reshape.82, bf16[1,1536,384]{2,1,0:T(8,128)(2,1)} %param.9), kind=kOutput, calls=%fused_computation.8 | convolution fusion | flops 603979776 | bytes 3538944 | tf_op jit(solution)/shard_map/dot_general | solution.py:16
  138.8 0.0 copy-done
  138.8 4.9 %convolution_convert_fusion = bf16[512,1536]{1,0:T(8,128)(2,1)} fusion(bf16[1,1536,384]{2,1,0:T(8,128)(2,1)S(1)} %copy-done, bf16[512,1536]{1,0:T(8,128)(2,1)} %reshape.82, bf16[1,1536,384]{2,1,0:T(8,128)(2,1)} %param.10, f32[512,384]{1,0:T(8,128)} %fusion.4), kind=kOutput, calls=%fused_computation.1 | convolution fusion | flops 1209925632 | bytes 6291456 | tf_op jit(solution)/shard_map/dot_general | solution.py:19
  143.7 4.5 %reshape.83 = bf16[4,64,2,1536]{3,2,1,0:T(2,128)(2,1)} reshape(bf16[512,1536]{1,0:T(8,128)(2,1)} %convolution_convert_fusion) | data formatting | bytes 3145728 | tf_op jit(solution)/shard_map/reshape | solution.py:50
  148.2 4.6 %all-to-all-start.2 = ((bf16[4,64,2,1536]{3,2,1,0:T(2,128)(2,1)}), bf16[4,64,2,1536]{3,2,1,0:T(2,128)(2,1)}, u32[]{:S(2)}, u32[]{:S(2)}) async-start(bf16[4,64,2,1536]{3,2,1,0:T(2,128)(2,1)} %reshape.83), calls=%async_computation.2 | async-start | bytes 3145728 | tf_op jit(solution)/shard_map/all_to_all | solution.py:51
  152.8 0.1 copy.48
  153.0 0.6 convert_reduce_fusion
  156.3 0.0 copy-start.1
  156.3 14.9 %all-to-all-done.2 = bf16[4,64,2,1536]{3,2,1,0:T(2,128)(2,1)} async-done(((bf16[4,64,2,1536]{3,2,1,0:T(2,128)(2,1)}), bf16[4,64,2,1536]{3,2,1,0:T(2,128)(2,1)}, u32[]{:S(2)}, u32[]{:S(2)}) %all-to-all-start.2) | async-done | bytes 1572896 | tf_op jit(solution)/shard_map/all_to_all | solution.py:51
  171.1 3.3 %reduce_sum.45 = bf16[64,2,1536]{2,1,0:T(2,128)(2,1)S(1)} reduce(bf16[4,64,2,1536]{3,2,1,0:T(2,128)(2,1)} %all-to-all-done.2, bf16[]{:T(256)} %constant.55.clone.1), dimensions={0}, to_apply=%region_4.5 | reduce | flops 589824 | bytes 1966082 | tf_op jit(solution)/shard_map/reduce_sum | solution.py:52
  174.4 1.2 pad_maximum_fusion
  175.6 7.5 %all-to-all-start.3 = ((bf16[64,2,1664]{2,1,0:T(2,128)(2,1)}), bf16[64,2,1664]{2,1,0:T(2,128)(2,1)S(1)}, u32[]{:S(2)}, u32[]{:S(2)}) async-start(bf16[64,2,1664]{2,1,0:T(2,128)(2,1)} %pad_maximum_fusion), calls=%async_computation.3 | async-start | bytes 851968 | tf_op jit(solution)/shard_map/all_to_all | solution.py:57
  183.2 0.1 mul.57
  183.3 0.0 copy-done.1
  183.3 0.1 copy.40
  183.4 55.5 %all-to-all-done.3 = bf16[64,2,1664]{2,1,0:T(2,128)(2,1)S(1)} async-done(((bf16[64,2,1664]{2,1,0:T(2,128)(2,1)}), bf16[64,2,1664]{2,1,0:T(2,128)(2,1)S(1)}, u32[]{:S(2)}, u32[]{:S(2)}) %all-to-all-start.3) | async-done | bytes 426016 | tf_op jit(solution)/shard_map/all_to_all | solution.py:57
  238.9 0.2 reshape.84
  239.1 0.8 gather_fusion
  239.8 0.1 fusion.14
  239.9 0.1 reshape.85
  240.1 0.1 copy.49
  240.2 0.5 add_bitcast_fusion
  240.7 0.9 multiply_reduce_fusion
  (12 shorter events, 0.2 us)
Async XLA Ops:
  0.6 138.2 %copy-start = (bf16[1,1536,384]{2,1,0:T(8,128)(2,1)S(1)}, bf16[1,1536,384]{2,1,0:T(8,128)(2,1)}, u32[]{:S(2)}) copy-start(bf16[1,1536,384]{2,1,0:T(8,128)(2,1)} %param.11) | copy-start | bytes 3538948
  148.2 22.9 %all-to-all-start.2 = ((bf16[4,64,2,1536]{3,2,1,0:T(2,128)(2,1)}), bf16[4,64,2,1536]{3,2,1,0:T(2,128)(2,1)}, u32[]{:S(2)}, u32[]{:S(2)}) async-start(bf16[4,64,2,1536]{3,2,1,0:T(2,128)(2,1)} %reshape.83), calls=%async_computation.2 | async-start | bytes 3145728 | tf_op jit(solution)/shard_map/all_to_all | solution.py:51
  156.3 27.0 %copy-start.1 = (f32[16,4]{0,1:T(4,128)S(1)}, f32[16,4]{0,1:T(4,128)}, u32[]{:S(2)}) copy-start(f32[16,4]{0,1:T(4,128)} %param.8) | copy-start | bytes 772
  175.6 63.3 %all-to-all-start.3 = ((bf16[64,2,1664]{2,1,0:T(2,128)(2,1)}), bf16[64,2,1664]{2,1,0:T(2,128)(2,1)S(1)}, u32[]{:S(2)}, u32[]{:S(2)}) async-start(bf16[64,2,1664]{2,1,0:T(2,128)(2,1)} %pad_maximum_fusion), calls=%async_computation.3 | async-start | bytes 851968 | tf_op jit(solution)/shard_map/all_to_all | solution.py:57

commit v2 on v1

--- a/solution.py
+++ b/solution.py
@@ -42,7 +42,7 @@
     outgoing = jnp.where(empty[:, None] & first[None, :], EMPTY, outgoing)
     outgoing = outgoing.astype(jnp.bfloat16).reshape(experts, capacity, model_width)
     arrived = lax.all_to_all(outgoing, ("ep", "dp"), split_axis=0, concat_axis=0, tiled=True)
-    fragment = copy_for_each(arrived, "tp")
+    fragment = copy_for_each(arrived.reshape(-1, model_width), "tp")
     load = jnp.sum((fragment[..., 0] < EMPTY - 1).astype(jnp.int32))
     partial_value = expert_apply(
         fragment.reshape(-1, model_width), w_gate[0], w_up[0], w_down[0]
@@ -51,9 +51,9 @@
     terms = lax.all_to_all(partial_terms, "tp", split_axis=0, concat_axis=0, tiled=True)
     finished = jnp.sum(terms.astype(jnp.float32), axis=0).astype(jnp.bfloat16)
     digits = jnp.where(jnp.arange(128) == 0, load // DIGIT, load % DIGIT).astype(jnp.bfloat16)
-    finished = jnp.concatenate(
-        [finished, jnp.broadcast_to(digits, (experts, capacity, 128))], axis=2
-    )
+    digits = jnp.broadcast_to(digits, (finished.shape[0], 128))
+    finished = jnp.concatenate([finished, digits], axis=1)
+    finished = finished.reshape(experts, capacity, -1)
     returned = lax.all_to_all(finished, ("ep", "dp"), split_axis=0, concat_axis=0, tiled=True)
     digits = returned[:, 0, model_width : model_width + 2].astype(jnp.int32)
     expert_loads = digits[:, 0] * DIGIT + digits[:, 1]

time: 242 us -> 229 us (0.946)
  local copies, waits for them, and re-layouts: 14.8 us -> 5.64 us
  other arithmetic: 7.2 us -> 4.46 us
    reshape x2 -> x3, local copies, waits for them, and re-layouts: 9.14 us -> 1.28 us  [the longest x1 0.91 us: per_device(): finished = finished.reshape(experts, capacity, -1)]
where the time goes in v2:
time: 229 us
  blocking collectives  124 us (54%)
  waiting for transfers between devices  70.7 us (31%)
  starting transfers between devices  12 us (5%)
  matrix products  8.52 us (4%)
  local copies, waits for them, and re-layouts  5.64 us (2%)
  other arithmetic  4.46 us (2%)
  between operations  3.43 us (1%)
    all_to_all x1, blocking collectives, per_device(): lax.all_to_all(outgoing, ('ep', 'dp'), split_axis=0, concat_axis=0, tiled...  100 us
    all_to_all x1, waiting for transfers between devices, per_device(): lax.all_to_all(finished, ('ep', 'dp'), split_axis=0, concat_axis=0, tiled...  55.5 us
    all_to_all x1, blocking collectives, copy_for_each(): return lax.all_to_all(copies, axis, split_axis=0, concat_axis=0, tiled=True)  24 us
    all_to_all x1, waiting for transfers between devices, per_device(): lax.all_to_all(partial_terms, 'tp', split_axis=0, concat_axis=0, tiled=True)  15.2 us
    all_to_all x1, starting transfers between devices, per_device(): lax.all_to_all(finished, ('ep', 'dp'), split_axis=0, concat_axis=0, tiled...  7.55 us
    dot_general x1, matrix products, expert_apply(): lax.dot_general(hidden, down_part, (((1,), (1,)), ((), ())), preferred_el...  4.7 us
  transfers between devices with their start and end apart: 2, of which 2 were waited for; matrix products, arithmetic and copies ran while one was open for 0% of the time, Pallas kernels for 0%

profile of v2, /device:TPU:40, one launch (start us, length us, event | category | flops | bytes accessed | tf_op | source)
XLA Modules:
  0.0 228.8 jit_solution(3936102065912471014)
XLA Ops:
  0.6 0.0 copy-start
  0.7 0.9 copy.55
  1.5 0.1 reshape.86
  1.6 0.1 fusion.17
  1.7 0.1 reduce_window_sum.11
  1.8 0.2 select_reduce_fusion
  2.0 0.1 reduce_sum.44
  2.1 0.1 copy.57
  2.1 0.1 fusion.16
  2.3 1.1 fusion
  3.4 0.1 reshape.87
  3.5 100.1 %all_to_all.20 = bf16[64,2,1536]{2,1,0:T(2,128)(2,1)S(1)} all-to-all(bf16[64,2,1536]{2,1,0:T(2,128)(2,1)S(1)} %reshape.87), channel_id=1, replica_groups=mesh['groups'=2,'ep'=32,'tp'=4,'dp'=2] {'ep','dp'}, dimensions={0} | all-to-all | bytes 786432 | tf_op jit(solution)/shard_map/all_to_all | solution.py:44
  103.6 0.1 reshape.88
  103.7 0.2 copy.58
  104.0 0.2 broadcast_in_dim.35
  104.2 24.0 %all_to_all.21 = bf16[4,128,1536]{1,2,0:T(8,128)(2,1)S(1)} all-to-all(bf16[4,128,1536]{1,2,0:T(8,128)(2,1)S(1)} %broadcast_in_dim.35), channel_id=1, replica_groups=mesh['groups'=2,'ep'=32,'tp'=4,'dp'=2] {'tp'}, dimensions={0} | all-to-all | bytes 3145728 | tf_op jit(solution)/shard_map/all_to_all | solution.py:12
  128.2 1.6 copy.59
  129.8 2.7 %fusion.4 = f32[512,384]{1,0:T(8,128)S(1)} fusion(bf16[512,1536]{1,0:T(8,128)(2,1)} %bitcast.30, bf16[1,1536,384]{2,1,0:T(8,128)(2,1)} %param.9), kind=kOutput, calls=%fused_computation.8 | convolution fusion | flops 603979776 | bytes 3538944 | tf_op jit(solution)/shard_map/dot_general | solution.py:16
  132.5 0.0 copy-done
  132.5 4.7 %convolution_convert_fusion = bf16[512,1536]{1,0:T(8,128)(2,1)} fusion(bf16[1,1536,384]{2,1,0:T(8,128)(2,1)S(1)} %copy-done, bf16[512,1536]{1,0:T(8,128)(2,1)} %bitcast.31, bf16[1,1536,384]{2,1,0:T(8,128)(2,1)} %param.10, f32[512,384]{1,0:T(8,128)S(1)} %fusion.4), kind=kOutput, calls=%fused_computation.1 | convolution fusion | flops 1209925632 | bytes 6291456 | tf_op jit(solution)/shard_map/dot_general | solution.py:19
  137.2 4.4 %all-to-all-start.2 = ((bf16[4,128,1536]{2,1,0:T(8,128)(2,1)}), bf16[4,128,1536]{2,1,0:T(8,128)(2,1)}, u32[]{:S(2)}, u32[]{:S(2)}) async-start(bf16[4,128,1536]{2,1,0:T(8,128)(2,1)} %bitcast.29), calls=%async_computation.2 | async-start | bytes 3145728 | tf_op jit(solution)/shard_map/all_to_all | solution.py:51
  141.7 0.6 reduce_sum.46
  144.9 15.2 %all-to-all-done.2 = bf16[4,128,1536]{2,1,0:T(8,128)(2,1)} async-done(((bf16[4,128,1536]{2,1,0:T(8,128)(2,1)}), bf16[4,128,1536]{2,1,0:T(8,128)(2,1)}, u32[]{:S(2)}, u32[]{:S(2)}) %all-to-all-start.2) | async-done | bytes 1572896 | tf_op jit(solution)/shard_map/all_to_all | solution.py:51
  160.1 1.7 reduce_sum.45
  161.8 0.0 copy-start.1
  161.8 0.1 pad_maximum_fusion
  161.9 0.9 reshape.91
  162.8 7.6 %all-to-all-start.3 = ((bf16[64,2,1664]{2,1,0:T(2,128)(2,1)}), bf16[64,2,1664]{2,1,0:T(2,128)(2,1)S(1)}, u32[]{:S(2)}, u32[]{:S(2)}) async-start(bf16[64,2,1664]{2,1,0:T(2,128)(2,1)} %reshape.91), calls=%async_computation.3 | async-start | bytes 851968 | tf_op jit(solution)/shard_map/all_to_all | solution.py:57
  170.4 0.1 mul.57
  170.5 0.0 copy-done.1
  170.5 0.1 copy.54
  170.6 55.5 %all-to-all-done.3 = bf16[64,2,1664]{2,1,0:T(2,128)(2,1)S(1)} async-done(((bf16[64,2,1664]{2,1,0:T(2,128)(2,1)}), bf16[64,2,1664]{2,1,0:T(2,128)(2,1)S(1)}, u32[]{:S(2)}, u32[]{:S(2)}) %all-to-all-start.3) | async-done | bytes 426016 | tf_op jit(solution)/shard_map/all_to_all | solution.py:57
  226.1 0.2 reshape.92
  226.3 0.8 gather_fusion
  227.0 0.1 fusion.14
  227.1 0.1 reshape.93
  227.3 0.1 copy.62
  227.4 0.5 add_bitcast_fusion
  227.9 0.9 multiply_reduce_fusion
  (11 shorter events, 0.1 us)
Async XLA Ops:
  0.6 131.9 %copy-start = (bf16[1,1536,384]{2,1,0:T(8,128)(2,1)S(1)}, bf16[1,1536,384]{2,1,0:T(8,128)(2,1)}, u32[]{:S(2)}) copy-start(bf16[1,1536,384]{2,1,0:T(8,128)(2,1)} %param.11) | copy-start | bytes 3538948
  137.2 22.9 %all-to-all-start.2 = ((bf16[4,128,1536]{2,1,0:T(8,128)(2,1)}), bf16[4,128,1536]{2,1,0:T(8,128)(2,1)}, u32[]{:S(2)}, u32[]{:S(2)}) async-start(bf16[4,128,1536]{2,1,0:T(8,128)(2,1)} %bitcast.29), calls=%async_computation.2 | async-start | bytes 3145728 | tf_op jit(solution)/shard_map/all_to_all | solution.py:51
  161.8 8.7 %copy-start.1 = (f32[16,4]{0,1:T(4,128)S(1)}, f32[16,4]{0,1:T(4,128)}, u32[]{:S(2)}) copy-start(f32[16,4]{0,1:T(4,128)} %param.8) | copy-start | bytes 772
  162.8 63.3 %all-to-all-start.3 = ((bf16[64,2,1664]{2,1,0:T(2,128)(2,1)}), bf16[64,2,1664]{2,1,0:T(2,128)(2,1)S(1)}, u32[]{:S(2)}, u32[]{:S(2)}) async-start(bf16[64,2,1664]{2,1,0:T(2,128)(2,1)} %reshape.91), calls=%async_computation.3 | async-start | bytes 851968 | tf_op jit(solution)/shard_map/all_to_all | solution.py:57

commit v3 on v2

--- a/solution.py
+++ b/solution.py
@@ -1,24 +1,80 @@
 import jax
 import jax.numpy as jnp
 from jax import lax
+from jax.experimental import pallas as pl
+from jax.experimental.pallas import tpu as pltpu
 from jax.sharding import PartitionSpec as P
 
 EMPTY = 8.0
 DIGIT = 64
+SUBLANES, LANES = 8, 128
 
 
-def copy_for_each(array, axis):
-    copies = jnp.broadcast_to(array, (lax.axis_size(axis), *array.shape))
-    return lax.all_to_all(copies, axis, split_axis=0, concat_axis=0, tiled=True)
+def shifted(array, axis, step):
+    size = lax.axis_size(axis)
+    return lax.ppermute(array, axis, [(i, (i + step) % size) for i in range(size)])
 
 
-def expert_apply(token_rows, gate_part, up_part, down_part):
-    gate_value = jnp.dot(token_rows, gate_part, preferred_element_type=jnp.float32)
-    up_value = jnp.dot(token_rows, up_part, preferred_element_type=jnp.float32)
+def expert_kernel(rows_ref, gate_ref, up_ref, down_ref, out_ref, held_ref):
+    rows = rows_ref[...]
+    gate_value = jnp.dot(rows, gate_ref[0], preferred_element_type=jnp.float32)
+    up_value = jnp.dot(rows, up_ref[0], preferred_element_type=jnp.float32)
     hidden = (jax.nn.silu(gate_value) * up_value).astype(jnp.bfloat16)
-    return lax.dot_general(
-        hidden, down_part, (((1,), (1,)), ((), ())), preferred_element_type=jnp.float32
+    result = lax.dot_general(
+        hidden, down_ref[0], (((1,), (1,)), ((), ())), preferred_element_type=jnp.float32
     )
+    out_ref[...] = result.astype(out_ref.dtype)
+    held = (rows[:, :LANES].astype(jnp.float32) < EMPTY - 1).astype(jnp.float32)
+    held_ref[...] = jnp.broadcast_to(jnp.sum(held, axis=0, keepdims=True), held_ref.shape)
+
+
+def expert_apply(rows, gate_part, up_part, down_part, dtype):
+    count, width = rows.shape
+    hidden = gate_part.shape[2]
+    whole = pl.BlockSpec(memory_space=pltpu.VMEM)
+    return pl.pallas_call(
+        expert_kernel,
+        out_shape=(
+            jax.ShapeDtypeStruct((count, width), dtype),
+            jax.ShapeDtypeStruct((SUBLANES, LANES), jnp.float32),
+        ),
+        in_specs=[whole] * 4,
+        out_specs=(whole, whole),
+        cost_estimate=pl.CostEstimate(
+            flops=6 * count * width * hidden,
+            bytes_accessed=6 * width * hidden + 4 * count * width,
+            transcendentals=count * hidden,
+        ),
+        compiler_params=pltpu.CompilerParams(vmem_limit_bytes=16 * 2**20),
+    )(rows, gate_part, up_part, down_part)
+
+
+def finish_kernel(own_ref, *refs):
+    *terms, out_ref = refs
+    half = len(terms) // 2
+    total = own_ref[...]
+    for term_ref in terms[:half]:
+        total = total + term_ref[...].astype(jnp.float32)
+    width = total.shape[1]
+    out_ref[:, :width] = total.astype(out_ref.dtype)
+    load = terms[half][:1, :1]
+    for held_ref in terms[half + 1 :]:
+        load = load + held_ref[:1, :1]
+    high = jnp.floor(load / DIGIT)
+    lane = lax.broadcasted_iota(jnp.int32, (total.shape[0], LANES), 1)
+    digits = jnp.where(lane == 0, high, load - high * DIGIT)
+    out_ref[:, width:] = digits.astype(out_ref.dtype)
+
+
+def finish(own, terms, held):
+    whole = pl.BlockSpec(memory_space=pltpu.VMEM)
+    return pl.pallas_call(
+        finish_kernel,
+        out_shape=jax.ShapeDtypeStruct((own.shape[0], own.shape[1] + LANES), jnp.bfloat16),
+        in_specs=[whole] * (1 + len(terms) + len(held)),
+        out_specs=whole,
+        compiler_params=pltpu.CompilerParams(vmem_limit_bytes=16 * 2**20),
+    )(own, *terms, *held)
 
 
 def per_device(tokens, expert_ids, gate_weights, w_gate, w_up, w_down):
@@ -42,17 +98,16 @@
     outgoing = jnp.where(empty[:, None] & first[None, :], EMPTY, outgoing)
     outgoing = outgoing.astype(jnp.bfloat16).reshape(experts, capacity, model_width)
     arrived = lax.all_to_all(outgoing, ("ep", "dp"), split_axis=0, concat_axis=0, tiled=True)
-    fragment = copy_for_each(arrived.reshape(-1, model_width), "tp")
-    load = jnp.sum((fragment[..., 0] < EMPTY - 1).astype(jnp.int32))
-    partial_value = expert_apply(
-        fragment.reshape(-1, model_width), w_gate[0], w_up[0], w_down[0]
-    ).astype(jnp.bfloat16)
-    partial_terms = partial_value.reshape(fragment.shape)
-    terms = lax.all_to_all(partial_terms, "tp", split_axis=0, concat_axis=0, tiled=True)
-    finished = jnp.sum(terms.astype(jnp.float32), axis=0).astype(jnp.bfloat16)
-    digits = jnp.where(jnp.arange(128) == 0, load // DIGIT, load % DIGIT).astype(jnp.bfloat16)
-    digits = jnp.broadcast_to(digits, (finished.shape[0], 128))
-    finished = jnp.concatenate([finished, digits], axis=1)
+    arrived = arrived.reshape(-1, model_width)
+    steps = (1, lax.axis_size("tp") - 1, *range(2, lax.axis_size("tp") - 1))
+    rows = [shifted(arrived, "tp", step) for step in steps]
+    total, load = expert_apply(arrived, w_gate, w_up, w_down, jnp.float32)
+    loads, terms = [load], []
+    for step, received in zip(steps, rows, strict=True):
+        partial_value, load = expert_apply(received, w_gate, w_up, w_down, jnp.bfloat16)
+        loads.append(load)
+        terms.append(shifted(partial_value, "tp", -step))
+    finished = finish(total, terms, loads)
     finished = finished.reshape(experts, capacity, -1)
     returned = lax.all_to_all(finished, ("ep", "dp"), split_axis=0, concat_axis=0, tiled=True)
     digits = returned[:, 0, model_width : model_width + 2].astype(jnp.int32)

time: 229 us -> 213 us (0.930)
  blocking collectives: 124 us -> 100 us
  starting transfers between devices: 12 us -> 34.9 us
  matrix products: 8.52 us -> 0.31 us
  waiting for transfers between devices: 70.7 us -> 64.6 us
  Pallas kernels: 0 us -> 4.26 us
  between operations: 3.43 us -> 0.89 us
  other arithmetic: 4.46 us -> 2.07 us
    ppermute x0 -> x6, starting transfers between devices: none -> 28.5 us  [shifted(): lax.ppermute(array, axis, [(i, (i + step) % size) for i in range(size)])]
    all_to_all x1 -> x0, blocking collectives: 24 us -> none  [copy_for_each(): return lax.all_to_all(copies, axis, split_axis=0, concat_axis=0, tiled=True)]
    all_to_all x1 -> x0, waiting for transfers between devices: 15.2 us -> none  [per_device(): lax.all_to_all(partial_terms, 'tp', split_axis=0, concat_axis=0, tiled=True)]
    ppermute x0 -> x6, waiting for transfers between devices: none -> 9.01 us  [shifted(): lax.ppermute(array, axis, [(i, (i + step) % size) for i in range(size)])]
    dot_general x2 -> x0, matrix products: 7.41 us -> none  [the longest x1 4.7 us: expert_apply(): lax.dot_general(hidden, down_part, (((1,), (1,)), ((), ())), preferred_el...]
    all_to_all x1 -> x0, starting transfers between devices: 4.42 us -> none  [per_device(): lax.all_to_all(partial_terms, 'tp', split_axis=0, concat_axis=0, tiled=True)]
    pallas_call x0 -> x5, Pallas kernels: none -> 4.26 us  [the longest x4 3.91 us: expert_apply(): pl.pallas_call(expert_kernel, out_shape=(jax.ShapeDtypeStruct((count, wid...]
    reduce_sum x2 -> x0, other arithmetic: 2.3 us -> none  [the longest x1 1.66 us: per_device(): finished = jnp.sum(terms.astype(jnp.float32), axis=0).astype(jnp.bfloat16)]
  transfers between devices with their start and end apart: 2 -> 7, of which waited for: 2 -> 4; matrix products, arithmetic and copies ran while one was open for 0% -> 0% of each run, Pallas kernels for 0% -> 2%
where the time goes in v3:
time: 213 us; the launch traced here: 212 us
  blocking collectives  100 us (47%)
  waiting for transfers between devices  64.6 us (30%)
  starting transfers between devices  34.9 us (16%)
  local copies, waits for them, and re-layouts  4.83 us (2%)
  Pallas kernels  4.26 us (2%)
    all_to_all x1, blocking collectives, per_device(): lax.all_to_all(outgoing, ('ep', 'dp'), split_axis=0, concat_axis=0, tiled...  100 us
    all_to_all x1, waiting for transfers between devices, per_device(): lax.all_to_all(finished, ('ep', 'dp'), split_axis=0, concat_axis=0, tiled...  55.6 us
    ppermute x6, starting transfers between devices, shifted(): lax.ppermute(array, axis, [(i, (i + step) % size) for i in range(size)])  28.5 us
    ppermute x6, waiting for transfers between devices, shifted(): lax.ppermute(array, axis, [(i, (i + step) % size) for i in range(size)])  9.01 us
    all_to_all x1, starting transfers between devices, per_device(): lax.all_to_all(finished, ('ep', 'dp'), split_axis=0, concat_axis=0, tiled...  6.49 us
  transfers between devices with their start and end apart: 7, of which 4 were waited for; matrix products, arithmetic and copies ran while one was open for 0% of the time, Pallas kernels for 2%

profile of v3, /device:TPU:40, one launch (start us, length us, event | category | flops | bytes accessed | tf_op | source)
XLA Modules:
  0.0 212.1 jit_solution(4686707261211410088)
XLA Ops:
  0.6 0.0 copy-start
  0.7 0.8 copy.28
  1.4 0.1 reshape.77
  1.5 0.1 fusion.4
  1.6 0.1 reduce_window_sum.11
  1.7 0.2 select_reduce_fusion
  1.9 0.1 reduce_sum.23
  2.0 0.1 copy.30
  2.0 0.1 fusion.3
  2.2 0.0 copy-done
  2.2 0.0 copy-start.2
  2.2 0.3 fusion
  2.5 0.0 copy-start.1
  2.5 0.1 reshape.78
  2.7 100.2 %all_to_all.10 = bf16[64,2,1536]{2,1,0:T(2,128)(2,1)S(1)} all-to-all(bf16[64,2,1536]{2,1,0:T(2,128)(2,1)S(1)} %reshape.78), channel_id=1, replica_groups=mesh['groups'=2,'ep'=32,'tp'=4,'dp'=2] {'ep','dp'}, dimensions={0} | all-to-all | bytes 786432 | tf_op jit(solution)/shard_map/all_to_all | solution.py:100
  102.9 0.1 reshape.79.rows_ref
  103.0 3.6 %collective-permute-start = (bf16[128,1536]{1,0:T(8,128)(2,1)S(1)}, bf16[128,1536]{1,0:T(8,128)(2,1)S(1)}, u32[]{:S(2)}, u32[]{:S(2)}) collective-permute-start(bf16[128,1536]{1,0:T(8,128)(2,1)S(1)} %reshape.79.rows_ref), channel_id=1, source_target_pairs={{0,2},{2,4},{4,6},{6,0},{1,3},{3,5},{5,7},{7,1},{8,10},{10,12},{12... | collective-permute-start | bytes 1179656 | tf_op jit(solution)/shard_map/ppermute | solution.py:15
  106.6 3.6 %collective-permute-start.2 = (bf16[128,1536]{1,0:T(8,128)(2,1)S(1)}, bf16[128,1536]{1,0:T(8,128)(2,1)S(1)}, u32[]{:S(2)}, u32[]{:S(2)}) collective-permute-start(bf16[128,1536]{1,0:T(8,128)(2,1)S(1)} %reshape.79.rows_ref), channel_id=1, source_target_pairs={{0,6},{2,0},{4,2},{6,4},{1,7},{3,1},{5,3},{7,5},{8,14},{10,8},{12,... | collective-permute-start | bytes 1179656 | tf_op jit(solution)/shard_map/ppermute | solution.py:15
  110.2 4.0 %collective-permute-start.4 = (bf16[128,1536]{1,0:T(8,128)(2,1)S(1)}, bf16[128,1536]{1,0:T(8,128)(2,1)S(1)}, u32[]{:S(2)}, u32[]{:S(2)}) collective-permute-start(bf16[128,1536]{1,0:T(8,128)(2,1)S(1)} %reshape.79.rows_ref), channel_id=1, source_target_pairs={{0,4},{2,6},{4,0},{6,2},{1,5},{3,7},{5,1},{7,3},{8,12},{10,14},{12... | collective-permute-start | bytes 1179656 | tf_op jit(solution)/shard_map/ppermute | solution.py:15
  114.2 3.0 %collective-permute-done.rows_ref = bf16[128,1536]{1,0:T(8,128)(2,1)S(1)} collective-permute-done((bf16[128,1536]{1,0:T(8,128)(2,1)S(1)}, bf16[128,1536]{1,0:T(8,128)(2,1)S(1)}, u32[]{:S(2)}, u32[]{:S(2)}) %collective-permute-start) | collective-permute-done | bytes 393248 | tf_op jit(solution)/shard_map/ppermute | solution.py:15
  117.2 1.3 copy-done.3
  118.5 1.0 shard_map.78
  119.4 4.9 %collective-permute-start.1 = (bf16[128,1536]{1,0:T(8,128)(2,1)S(1)}, bf16[128,1536]{1,0:T(8,128)(2,1)S(1)}, u32[]{:S(2)}, u32[]{:S(2)}) collective-permute-start(bf16[128,1536]{1,0:T(8,128)(2,1)S(1)} %get-tuple-element.11), channel_id=1, source_target_pairs={{0,6},{2,0},{4,2},{6,4},{1,7},{3,1},{5,3},{7,5},{8,14},{10,8},{12,... | collective-permute-start | bytes 1179656 | tf_op jit(solution)/shard_map/ppermute | solution.py:15
  124.3 0.0 collective-permute-done.2.rows_ref
  124.3 1.0 shard_map.79
  125.3 0.0 copy-start.4
  125.3 2.1 collective-permute-start.3
  127.4 0.0 collective-permute-done.4.rows_ref
  127.4 1.0 shard_map.80
  128.4 10.4 %collective-permute-start.5 = (bf16[128,1536]{1,0:T(8,128)(2,1)S(1)}, bf16[128,1536]{1,0:T(8,128)(2,1)S(1)}, u32[]{:S(2)}, u32[]{:S(2)}) collective-permute-start(bf16[128,1536]{1,0:T(8,128)(2,1)S(1)} %get-tuple-element.13), channel_id=1, source_target_pairs={{0,4},{2,6},{4,0},{6,2},{1,5},{3,7},{5,1},{7,3},{8,12},{10,14},{12... | collective-permute-start | bytes 1179656 | tf_op jit(solution)/shard_map/ppermute | solution.py:15
  138.8 1.0 shard_map.77
  139.8 0.0 collective-permute-done.1.refs_0_
  139.8 0.3 collective-permute-done.3.refs_1_
  140.1 5.7 %collective-permute-done.5.refs_2_ = bf16[128,1536]{1,0:T(8,128)(2,1)S(1)} collective-permute-done((bf16[128,1536]{1,0:T(8,128)(2,1)S(1)}, bf16[128,1536]{1,0:T(8,128)(2,1)S(1)}, u32[]{:S(2)}, u32[]{:S(2)}) %collective-permute-start.5) | collective-permute-done | bytes 393248 | tf_op jit(solution)/shard_map/ppermute | solution.py:15
  145.8 0.3 shard_map.81
  146.2 0.0 copy-start.5
  146.2 0.9 reshape.80
  147.1 6.5 %all-to-all-start.1 = ((bf16[64,2,1664]{2,1,0:T(2,128)(2,1)}), bf16[64,2,1664]{2,1,0:T(2,128)(2,1)S(1)}, u32[]{:S(2)}, u32[]{:S(2)}) async-start(bf16[64,2,1664]{2,1,0:T(2,128)(2,1)} %reshape.80), calls=%async_computation.1 | async-start | bytes 851968 | tf_op jit(solution)/shard_map/all_to_all | solution.py:112
  153.6 0.1 mul.48
  153.7 0.1 copy.27
  153.8 55.6 %all-to-all-done.1 = bf16[64,2,1664]{2,1,0:T(2,128)(2,1)S(1)} async-done(((bf16[64,2,1664]{2,1,0:T(2,128)(2,1)}), bf16[64,2,1664]{2,1,0:T(2,128)(2,1)S(1)}, u32[]{:S(2)}, u32[]{:S(2)}) %all-to-all-start.1) | async-done | bytes 426016 | tf_op jit(solution)/shard_map/all_to_all | solution.py:112
  209.4 0.2 reshape.81
  209.6 0.8 gather_fusion
  210.3 0.1 fusion.1
  210.4 0.1 reshape.82
  210.6 0.1 copy.32
  210.7 0.5 add_bitcast_fusion
  211.2 0.9 multiply_reduce_fusion
  (13 shorter events, 0.1 us)
Async XLA Ops:
  0.6 1.5 copy-start
  2.2 115.0 %copy-start.2 = (bf16[1,1536,384]{2,1,0:T(8,128)(2,1)S(1)}, bf16[1,1536,384]{2,1,0:T(8,128)(2,1)}, u32[]{:S(2)}) copy-start(bf16[1,1536,384]{2,1,0:T(8,128)(2,1)} %up_ref.7) | copy-start | bytes 3538948
  2.5 114.7 %copy-start.1 = (bf16[1,1536,384]{2,1,0:T(8,128)(2,1)S(1)}, bf16[1,1536,384]{2,1,0:T(8,128)(2,1)}, u32[]{:S(2)}) copy-start(bf16[1,1536,384]{2,1,0:T(8,128)(2,1)} %gate_ref.7) | copy-start | bytes 3538948
  103.0 14.2 %collective-permute-start = (bf16[128,1536]{1,0:T(8,128)(2,1)S(1)}, bf16[128,1536]{1,0:T(8,128)(2,1)S(1)}, u32[]{:S(2)}, u32[]{:S(2)}) collective-permute-start(bf16[128,1536]{1,0:T(8,128)(2,1)S(1)} %reshape.79.rows_ref), channel_id=1, source_target_pairs={{0,2},{2,4},{4,6},{6,0},{1,3},{3,5},{5,7},{7,1},{8,10},{10,12},{12... | collective-permute-start | bytes 1179656 | tf_op jit(solution)/shard_map/ppermute | solution.py:15
  106.6 17.7 %collective-permute-start.2 = (bf16[128,1536]{1,0:T(8,128)(2,1)S(1)}, bf16[128,1536]{1,0:T(8,128)(2,1)S(1)}, u32[]{:S(2)}, u32[]{:S(2)}) collective-permute-start(bf16[128,1536]{1,0:T(8,128)(2,1)S(1)} %reshape.79.rows_ref), channel_id=1, source_target_pairs={{0,6},{2,0},{4,2},{6,4},{1,7},{3,1},{5,3},{7,5},{8,14},{10,8},{12,... | collective-permute-start | bytes 1179656 | tf_op jit(solution)/shard_map/ppermute | solution.py:15
  110.2 17.3 %collective-permute-start.4 = (bf16[128,1536]{1,0:T(8,128)(2,1)S(1)}, bf16[128,1536]{1,0:T(8,128)(2,1)S(1)}, u32[]{:S(2)}, u32[]{:S(2)}) collective-permute-start(bf16[128,1536]{1,0:T(8,128)(2,1)S(1)} %reshape.79.rows_ref), channel_id=1, source_target_pairs={{0,4},{2,6},{4,0},{6,2},{1,5},{3,7},{5,1},{7,3},{8,12},{10,14},{12... | collective-permute-start | bytes 1179656 | tf_op jit(solution)/shard_map/ppermute | solution.py:15
  117.2 1.3 copy-start.3
  119.4 20.3 %collective-permute-start.1 = (bf16[128,1536]{1,0:T(8,128)(2,1)S(1)}, bf16[128,1536]{1,0:T(8,128)(2,1)S(1)}, u32[]{:S(2)}, u32[]{:S(2)}) collective-permute-start(bf16[128,1536]{1,0:T(8,128)(2,1)S(1)} %get-tuple-element.11), channel_id=1, source_target_pairs={{0,6},{2,0},{4,2},{6,4},{1,7},{3,1},{5,3},{7,5},{8,14},{10,8},{12,... | collective-permute-start | bytes 1179656 | tf_op jit(solution)/shard_map/ppermute | solution.py:15
  125.3 13.5 %copy-start.4 = (bf16[1,1536,384]{2,1,0:T(8,128)(2,1)S(1)}, bf16[1,1536,384]{2,1,0:T(8,128)(2,1)}, u32[]{:S(2)}) copy-start(bf16[1,1536,384]{2,1,0:T(8,128)(2,1)} %down_ref.7) | copy-start | bytes 3538948
  125.3 14.8 %collective-permute-start.3 = (bf16[128,1536]{1,0:T(8,128)(2,1)S(1)}, bf16[128,1536]{1,0:T(8,128)(2,1)S(1)}, u32[]{:S(2)}, u32[]{:S(2)}) collective-permute-start(bf16[128,1536]{1,0:T(8,128)(2,1)S(1)} %get-tuple-element.12), channel_id=1, source_target_pairs={{0,2},{2,4},{4,6},{6,0},{1,3},{3,5},{5,7},{7,1},{8,10},{10,12},{12... | collective-permute-start | bytes 1179656 | tf_op jit(solution)/shard_map/ppermute | solution.py:15
  128.4 17.4 %collective-permute-start.5 = (bf16[128,1536]{1,0:T(8,128)(2,1)S(1)}, bf16[128,1536]{1,0:T(8,128)(2,1)S(1)}, u32[]{:S(2)}, u32[]{:S(2)}) collective-permute-start(bf16[128,1536]{1,0:T(8,128)(2,1)S(1)} %get-tuple-element.13), channel_id=1, source_target_pairs={{0,4},{2,6},{4,0},{6,2},{1,5},{3,7},{5,1},{7,3},{8,12},{10,14},{12... | collective-permute-start | bytes 1179656 | tf_op jit(solution)/shard_map/ppermute | solution.py:15
  146.2 7.5 %copy-start.5 = (f32[16,4]{0,1:T(4,128)S(1)}, f32[16,4]{0,1:T(4,128)}, u32[]{:S(2)}) copy-start(f32[16,4]{0,1:T(4,128)} %param.8) | copy-start | bytes 772
  147.1 62.3 %all-to-all-start.1 = ((bf16[64,2,1664]{2,1,0:T(2,128)(2,1)}), bf16[64,2,1664]{2,1,0:T(2,128)(2,1)S(1)}, u32[]{:S(2)}, u32[]{:S(2)}) async-start(bf16[64,2,1664]{2,1,0:T(2,128)(2,1)} %reshape.80), calls=%async_computation.1 | async-start | bytes 851968 | tf_op jit(solution)/shard_map/all_to_all | solution.py:112

commit v4 on v2

v4 whole, which is shorter than its diff:
```python
import jax
import jax.numpy as jnp
from jax import lax
from jax.experimental import pallas as pl
from jax.experimental.pallas import tpu as pltpu
from jax.sharding import Mesh
from jax.sharding import PartitionSpec as P

EMPTY = 8.0
DIGIT = 64
NEAR = 2
SLOTS = 2
BLOCK = NEAR * 2
LANES = 128

f32, bf16 = jnp.float32, jnp.bfloat16
WHOLE = pl.BlockSpec(memory_space=pltpu.VMEM)
PARAMS = pltpu.CompilerParams(vmem_limit_bytes=16 * 2**20)


def iota(shape, dim):
    return lax.broadcasted_iota(jnp.int32, shape, dim)


def column(row):
    shape = (row.shape[1], row.shape[1])
    return jnp.sum(jnp.where(iota(shape, 0) == iota(shape, 1), row, 0), axis=1, keepdims=True)


def placed(ids, lanes, expert, rank, values=None):
    count = ids.shape[1]
    named = jnp.zeros((count, lanes), f32)
    value = jnp.zeros((count, lanes), f32)
    for k in range(ids.shape[0]):
        hit = column(ids[k : k + 1, :].astype(f32)).astype(jnp.int32) == expert
        named = named + jnp.where(hit, 1.0, 0.0)
        if values is not None:
            value = value + jnp.where(hit, column(values[k : k + 1, :]), 0.0)
    earlier = jnp.where(iota((count, count), 1) < iota((count, count), 0), 1.0, 0.0)
    ranks = jnp.dot(earlier.astype(bf16), named.astype(bf16), preferred_element_type=f32)
    chosen = (named > 0.5) & (ranks.astype(jnp.int32) == rank)
    return jnp.where(chosen, named if values is None else value, 0.0)


def pack_kernel(
    tokens_ref, ids_ref, weights_ref, out_ref, high_ref, low_ref, ids, weights, token_sem, ids_sem, weights_sem
):
    count, width = tokens_ref.shape
    lanes = out_ref.shape[1] - width
    token_copy = pltpu.make_async_copy(tokens_ref, out_ref.at[:, pl.ds(0, width)], token_sem)
    ids_copy = pltpu.make_async_copy(ids_ref, ids, ids_sem)
    weights_copy = pltpu.make_async_copy(weights_ref, weights, weights_sem)
    ids_copy.start()
    weights_copy.start()
    token_copy.start()
    ids_copy.wait()
    weights_copy.wait()
    lane = iota((count, lanes), 1)
    half = lanes // SLOTS
    out_ref[:, width:] = placed(ids[...], lanes, lane % half, lane // half).astype(bf16)
    slot = lane // SLOTS
    far = half // BLOCK
    mix = placed(ids[...], lanes, slot % far * BLOCK + slot // far, lane % SLOTS, weights[...])
    high = mix.astype(bf16)
    high_ref[...] = high
    low_ref[...] = (mix - high.astype(f32)).astype(bf16)
    token_copy.wait()


def select_kernel(block_ref, gathered_ref, out_ref):
    copies, count, width = out_ref.shape
    lanes = gathered_ref.shape[1] - width
    tokens = gathered_ref.shape[0]
    experts = lanes // SLOTS
    far = count // (SLOTS * BLOCK)
    row = iota((lanes, count), 1)
    lane = iota((lanes, count), 0)
    expert = block_ref[0] * BLOCK + row // (far * SLOTS)
    pick = jnp.where(lane == row % SLOTS * experts + expert, 1.0, 0.0).astype(bf16)
    chosen = jnp.dot(gathered_ref[:, width:], pick, preferred_element_type=f32)
    source = iota((tokens, count), 0) // (tokens // far)
    mine = source == iota((tokens, count), 1) // SLOTS % far
    chosen = jnp.where(mine, chosen, 0.0).astype(bf16)
    contract = (((0,), (0,)), ((), ()))
    rows = lax.dot_general(chosen, gathered_ref[:, :width], contract, preferred_element_type=f32)
    held = lax.dot_general(
        chosen, jnp.ones((tokens, LANES), bf16), contract, preferred_element_type=f32
    )
    empty = (held < 0.5) & (iota((count, LANES), 1) == 0)
    start = jnp.where(empty, EMPTY, rows[:, :LANES]).astype(bf16)
    rest = rows[:, LANES:].astype(bf16)
    for copy in range(copies):
        out_ref[copy, :, :LANES] = start
        out_ref[copy, :, LANES:] = rest


def expert_kernel(peer_ref, rows_ref, gate_ref, up_ref, down_ref, out_ref):
    count = out_ref.shape[0]
    rows = rows_ref[pl.ds(pl.multiple_of(peer_ref[0] * count, count), count), :]
    gate_value = jnp.dot(rows, gate_ref[0], preferred_element_type=f32)
    up_value = jnp.dot(rows, up_ref[0], preferred_element_type=f32)
    hidden = (jax.nn.silu(gate_value) * up_value).astype(bf16)
    result = lax.dot_general(
        hidden, down_ref[0], (((1,), (1,)), ((), ())), preferred_element_type=f32
    )
    out_ref[...] = result.astype(out_ref.dtype)


def expert_apply(peer, rows, gate_part, up_part, down_part, count, dtype):
    width, hidden = rows.shape[1], gate_part.shape[2]
    return pl.pallas_call(
        expert_kernel,
        out_shape=jax.ShapeDtypeStruct((count, width), dtype),
        in_specs=[pl.BlockSpec(memory_space=pltpu.SMEM)] + [WHOLE] * 4,
        out_specs=WHOLE,
        cost_estimate=pl.CostEstimate(
            flops=6 * count * width * hidden,
            bytes_accessed=6 * width * hidden + 4 * count * width,
            transcendentals=count * hidden,
        ),
        compiler_params=PARAMS,
    )(peer, rows, gate_part, up_part, down_part)


def finish_kernel(rows_ref, own_ref, *refs):
    *terms, out_ref = refs
    total = own_ref[...]
    for term_ref in terms:
        total = total + term_ref[...].astype(f32)
    width = total.shape[1]
    out_ref[:, :width] = total.astype(bf16)
    held = jnp.where(rows_ref[:, :LANES].astype(f32) < EMPTY - 1, 1.0, 0.0)
    load = jnp.sum(held, axis=0, keepdims=True)[:, :1]
    high = jnp.floor(load / DIGIT)
    lane = iota((total.shape[0], LANES), 1)
    out_ref[:, width:] = jnp.where(lane == 0, high, load - high * DIGIT).astype(bf16)


def mix_kernel(returned_ref, high_ref, low_ref, mixed_ref, loads_ref):
    width = mixed_ref.shape[1]
    count = returned_ref.shape[0]
    far = count // (SLOTS * BLOCK)
    rows = returned_ref[:, :width]
    mixed = jnp.dot(high_ref[...], rows, preferred_element_type=f32)
    mixed = mixed + jnp.dot(low_ref[...], rows, preferred_element_type=f32)
    mixed_ref[...] = mixed.astype(bf16)
    digits = returned_ref[:, width : width + LANES].astype(f32)
    load = digits[:, :1] * DIGIT + digits[:, 1:2]
    shape = (count, LANES)
    expert = iota(shape, 1)
    first = (expert % BLOCK * far + expert // BLOCK) * SLOTS
    load = jnp.where(iota(shape, 0) == first, load, 0.0)
    loads_ref[...] = jnp.sum(load, axis=0, keepdims=True).astype(jnp.int32)


def all_to_all(array, axis):
    return lax.all_to_all(array, axis, split_axis=0, concat_axis=0, tiled=True)


def shifted(array, axis, step):
    size = lax.axis_size(axis)
    return lax.ppermute(array, axis, [(i, (i + step) % size) for i in range(size)])


def per_device(tokens, expert_ids, gate_weights, w_gate, w_up, w_down):
    count, width = tokens.shape
    far, near = lax.axis_size("eh"), lax.axis_size("el")
    tp, dp = lax.axis_size("tp"), lax.axis_size("dp")
    experts = far * near * dp
    slots = experts * SLOTS
    steps = (*range(2, tp - 1), 1, tp - 1, 0)
    packed, high, low = pl.pallas_call(
        pack_kernel,
        out_shape=(
            jax.ShapeDtypeStruct((count, width + slots), bf16),
            jax.ShapeDtypeStruct((count, slots), bf16),
            jax.ShapeDtypeStruct((count, slots), bf16),
        ),
        in_specs=[pl.BlockSpec(memory_space=pl.ANY)] * 3,
        out_specs=(WHOLE,) * 3,
        scratch_shapes=[
            pltpu.VMEM((expert_ids.shape[1], count), jnp.int32),
            pltpu.VMEM((expert_ids.shape[1], count), f32),
            *[pltpu.SemaphoreType.DMA] * 3,
        ],
        compiler_params=PARAMS,
    )(tokens, expert_ids.T, gate_weights.T)
    me = lax.axis_index("tp").astype(jnp.int32)
    block = lax.axis_index("eh").astype(jnp.int32).reshape(1)
    peers = [((me + step) % tp).reshape(1) for step in steps]
    packed, block, *peers = lax.optimization_barrier((packed, block, *peers))
    gathered = lax.all_gather(packed, "eh", tiled=True)
    outgoing = pl.pallas_call(
        select_kernel,
        out_shape=jax.ShapeDtypeStruct((tp, slots, width), bf16),
        in_specs=[pl.BlockSpec(memory_space=pltpu.SMEM), WHOLE],
        out_specs=WHOLE,
        compiler_params=PARAMS,
    )(block, gathered)
    outgoing = outgoing.reshape(tp * near * dp, far * SLOTS, width)
    arrived = all_to_all(outgoing, ("tp", "el", "dp")).reshape(tp * slots, width)

    terms = []
    for turn, step in enumerate(steps[:-1]):
        partial_value = expert_apply(peers[turn], arrived, w_gate, w_up, w_down, slots, bf16)
        terms.append(shifted(partial_value, "tp", step))
    own = expert_apply(peers[-1], arrived, w_gate, w_up, w_down, slots, f32)
    finished = pl.pallas_call(
        finish_kernel,
        out_shape=jax.ShapeDtypeStruct((slots, width + LANES), bf16),
        in_specs=[WHOLE] * (2 + len(terms)),
        out_specs=WHOLE,
        compiler_params=PARAMS,
    )(arrived, own, *terms)
    returned = all_to_all(finished.reshape(experts, SLOTS, -1), ("el", "dp", "eh"))
    mixed, loads = pl.pallas_call(
        mix_kernel,
        out_shape=(
            jax.ShapeDtypeStruct((count, width), bf16),
            jax.ShapeDtypeStruct((1, LANES), jnp.int32),
        ),
        in_specs=[WHOLE] * 3,
        out_specs=(WHOLE, WHOLE),
        compiler_params=PARAMS,
    )(returned.reshape(slots, -1), high, low)
    return mixed, loads[0, :experts]


def solution(mesh):
    sizes = mesh.shape
    devices = mesh.devices.reshape(
        sizes["groups"], sizes["ep"] // NEAR, NEAR, sizes["tp"], sizes["dp"]
    )
    split = Mesh(devices, ("groups", "eh", "el", "tp", "dp"))
    token_spec = P(("groups", "eh", "el", "tp", "dp"), None)
    weight_spec = P(("eh", "el", "dp"), None, "tp")
    return jax.shard_map(
        per_device,
        mesh=split,
        in_specs=(token_spec,) * 3 + (weight_spec,) * 3,
        out_specs=(token_spec, P("groups")),
        check_vma=False,
    )
```

time: 229 us -> 205 us (0.90); the launches traced: 229 us -> 202 us
  waiting for transfers between devices: 70.7 us -> 11.2 us
  blocking collectives: 124 us -> 171 us
  matrix products: 8.52 us -> 0 us
  Pallas kernels: 0 us -> 5.95 us
  other arithmetic: 4.46 us -> 0 us
  between operations: 3.43 us -> 0.78 us
  local copies, waits for them, and re-layouts: 5.64 us -> 3 us
    all_gather x0 -> x1, blocking collectives: none -> 81 us  [per_device(): gathered = lax.all_gather(packed, 'eh', tiled=True)]
    all_to_all x2 -> x0, waiting for transfers between devices: 70.7 us -> none  [the longest x1 55.5 us: per_device(): lax.all_to_all(finished, ('ep', 'dp'), split_axis=0, concat_axis=0, tiled...]
    all_to_all x2, blocking collectives: 124 us -> 89.8 us  [all_to_all(): return lax.all_to_all(array, axis, split_axis=0, concat_axis=0, tiled=True)]
    all_to_all x2 -> x0, starting transfers between devices: 12 us -> none  [the longest x1 7.55 us: per_device(): lax.all_to_all(finished, ('ep', 'dp'), split_axis=0, concat_axis=0, tiled...]
    ppermute x0 -> x3, waiting for transfers between devices: none -> 11.2 us  [shifted(): lax.ppermute(array, axis, [(i, (i + step) % size) for i in range(size)])]
    ppermute x0 -> x3, starting transfers between devices: none -> 9.93 us  [shifted(): lax.ppermute(array, axis, [(i, (i + step) % size) for i in range(size)])]
    dot_general x3 -> x0, matrix products: 8.52 us -> none  [the longest x1 4.7 us: expert_apply(): lax.dot_general(hidden, down_part, (((1,), (1,)), ((), ())), preferred_el...]
    pallas_call x0 -> x8, Pallas kernels: none -> 5.95 us  [the longest x4 3.95 us: expert_apply(): pl.pallas_call(expert_kernel, out_shape=jax.ShapeDtypeStruct((count, widt...]
  transfers between devices with their start and end apart: 2 -> 3, of which waited for: 2 -> 2; matrix products, arithmetic and copies ran while one was open for 0% -> 0% of each run, Pallas kernels for 0% -> 0%
where the time goes in v4:
time: 205 us; the launch traced here: 202 us
  blocking collectives  171 us (83%)
  waiting for transfers between devices  11.2 us (5%)
  starting transfers between devices  9.93 us (5%)
  Pallas kernels  5.95 us (3%)
  local copies, waits for them, and re-layouts  3 us (1%)
    all_to_all x2, blocking collectives, all_to_all(): return lax.all_to_all(array, axis, split_axis=0, concat_axis=0, tiled=True)  89.8 us
    all_gather x1, blocking collectives, per_device(): gathered = lax.all_gather(packed, 'eh', tiled=True)  81 us
    ppermute x3, waiting for transfers between devices, shifted(): lax.ppermute(array, axis, [(i, (i + step) % size) for i in range(size)])  11.2 us
    ppermute x3, starting transfers between devices, shifted(): lax.ppermute(array, axis, [(i, (i + step) % size) for i in range(size)])  9.93 us
  transfers between devices with their start and end apart: 3, of which 2 were waited for; matrix products, arithmetic and copies ran while one was open for 0% of the time, Pallas kernels for 0%

profile of v4, /device:TPU:40, one launch (start us, length us, event | category | flops | bytes accessed | tf_op | source)
XLA Modules:
  0.0 201.7 jit_solution(14560440653860620404)
XLA Ops:
  0.7 0.0 copy-start.3
  0.7 0.8 copy-done.3
  1.5 0.0 copy-start.4
  1.5 0.7 copy-done.4
  2.2 0.0 copy-start.5
  2.2 0.7 copy-done.5
  2.8 0.3 shard_map.77
  3.1 81.0 %all_gather.3.gathered_ref = bf16[256,1664]{1,0:T(8,128)(2,1)S(1)} all-gather(bf16[16,1664]{1,0:T(8,128)(2,1)S(1)} %get-tuple-element.15), channel_id=1, replica_groups=mesh['groups'=2,'eh'=16,'el'=2,'tp'=4,'dp'=2] {'eh'}, dimensions={0}, use_global_device_ids=true | all-gather | bytes 905216 | tf_op jit(solution)/shard_map/all_gather | solution.py:192
  84.1 0.0 copy-start.2
  84.1 0.5 shard_map.78
  84.6 0.0 copy-start
  84.6 0.0 copy-start.1
  84.6 26.7 %all_to_all.10 = bf16[16,32,1536]{2,1,0:T(8,128)(2,1)S(1)} all-to-all(bf16[16,32,1536]{2,1,0:T(8,128)(2,1)S(1)} %bitcast.16), channel_id=1, replica_groups=mesh['groups'=2,'eh'=16,'el'=2,'tp'=4,'dp'=2] {'tp','el','dp'}, dimensions={0} | all-to-all | bytes 3145728 | tf_op jit(solution)/shard_map/all_to_all | solution.py:157
  111.3 0.0 copy-done.2
  111.3 0.0 copy-done
  111.3 0.0 copy-done.1
  111.3 1.0 shard_map.82
  112.3 1.0 shard_map.81
  113.3 1.0 shard_map.80
  114.3 2.8 %collective-permute-start = (bf16[128,1536]{1,0:T(8,128)(2,1)S(1)}, bf16[128,1536]{1,0:T(8,128)(2,1)S(1)}, u32[]{:S(2)}, u32[]{:S(2)}) collective-permute-start(bf16[128,1536]{1,0:T(8,128)(2,1)S(1)} %shard_map.80), channel_id=1, source_target_pairs={{0,4},{2,6},{4,0},{6,2},{1,5},{3,7},{5,1},{7,3},{8,12},{10,14},{12... | collective-permute-start | bytes 1179656 | tf_op jit(solution)/shard_map/ppermute | solution.py:162
  117.1 2.8 %collective-permute-start.1 = (bf16[128,1536]{1,0:T(8,128)(2,1)S(1)}, bf16[128,1536]{1,0:T(8,128)(2,1)S(1)}, u32[]{:S(2)}, u32[]{:S(2)}) collective-permute-start(bf16[128,1536]{1,0:T(8,128)(2,1)S(1)} %shard_map.81), channel_id=1, source_target_pairs={{0,2},{2,4},{4,6},{6,0},{1,3},{3,5},{5,7},{7,1},{8,10},{10,12},{12... | collective-permute-start | bytes 1179656 | tf_op jit(solution)/shard_map/ppermute | solution.py:162
  119.9 4.3 %collective-permute-start.2 = (bf16[128,1536]{1,0:T(8,128)(2,1)S(1)}, bf16[128,1536]{1,0:T(8,128)(2,1)S(1)}, u32[]{:S(2)}, u32[]{:S(2)}) collective-permute-start(bf16[128,1536]{1,0:T(8,128)(2,1)S(1)} %shard_map.82), channel_id=1, source_target_pairs={{0,6},{2,0},{4,2},{6,4},{1,7},{3,1},{5,3},{7,5},{8,14},{10,8},{12,... | collective-permute-start | bytes 1179656 | tf_op jit(solution)/shard_map/ppermute | solution.py:162
  124.2 1.0 shard_map.79.own_ref
  125.2 4.5 %collective-permute-done.refs_0_ = bf16[128,1536]{1,0:T(8,128)(2,1)S(1)} collective-permute-done((bf16[128,1536]{1,0:T(8,128)(2,1)S(1)}, bf16[128,1536]{1,0:T(8,128)(2,1)S(1)}, u32[]{:S(2)}, u32[]{:S(2)}) %collective-permute-start) | collective-permute-done | bytes 393248 | tf_op jit(solution)/shard_map/ppermute | solution.py:162
  129.7 6.7 %collective-permute-done.1.refs_1_ = bf16[128,1536]{1,0:T(8,128)(2,1)S(1)} collective-permute-done((bf16[128,1536]{1,0:T(8,128)(2,1)S(1)}, bf16[128,1536]{1,0:T(8,128)(2,1)S(1)}, u32[]{:S(2)}, u32[]{:S(2)}) %collective-permute-start.1) | collective-permute-done | bytes 393248 | tf_op jit(solution)/shard_map/ppermute | solution.py:162
  136.4 0.0 collective-permute-done.2.refs_2_
  136.4 0.4 shard_map.83
  136.8 0.2 reshape.38
  137.0 63.2 %all_to_all.11 = bf16[64,2,1664]{2,1,0:T(2,128)(2,1)S(1)} all-to-all(bf16[64,2,1664]{2,1,0:T(2,128)(2,1)S(1)} %reshape.38), channel_id=1, replica_groups=mesh['groups'=2,'eh'=16,'el'=2,'tp'=4,'dp'=2] {'el','dp','eh'}, dimensions={0} | all-to-all | bytes 851968 | tf_op jit(solution)/shard_map/all_to_all | solution.py:157
  200.2 0.2 reshape.39.returned_ref
  200.3 0.8 shard_map.84
  201.2 0.5 slice_bitcast_fusion
Async XLA Ops:
  0.7 0.8 copy-start.3
  1.5 0.7 copy-start.4
  2.2 0.7 copy-start.5
  84.1 27.2 %copy-start.2 = (bf16[1,1536,384]{2,1,0:T(8,128)(2,1)S(1)}, bf16[1,1536,384]{2,1,0:T(8,128)(2,1)}, u32[]{:S(2)}) copy-start(bf16[1,1536,384]{2,1,0:T(8,128)(2,1)} %down_ref.7) | copy-start | bytes 3538948
  84.6 26.7 %copy-start = (bf16[1,1536,384]{2,1,0:T(8,128)(2,1)S(1)}, bf16[1,1536,384]{2,1,0:T(8,128)(2,1)}, u32[]{:S(2)}) copy-start(bf16[1,1536,384]{2,1,0:T(8,128)(2,1)} %gate_ref.7) | copy-start | bytes 3538948
  84.6 26.7 %copy-start.1 = (bf16[1,1536,384]{2,1,0:T(8,128)(2,1)S(1)}, bf16[1,1536,384]{2,1,0:T(8,128)(2,1)}, u32[]{:S(2)}) copy-start(bf16[1,1536,384]{2,1,0:T(8,128)(2,1)} %up_ref.7) | copy-start | bytes 3538948
  114.3 15.5 %collective-permute-start = (bf16[128,1536]{1,0:T(8,128)(2,1)S(1)}, bf16[128,1536]{1,0:T(8,128)(2,1)S(1)}, u32[]{:S(2)}, u32[]{:S(2)}) collective-permute-start(bf16[128,1536]{1,0:T(8,128)(2,1)S(1)} %shard_map.80), channel_id=1, source_target_pairs={{0,4},{2,6},{4,0},{6,2},{1,5},{3,7},{5,1},{7,3},{8,12},{10,14},{12... | collective-permute-start | bytes 1179656 | tf_op jit(solution)/shard_map/ppermute | solution.py:162
  117.1 19.3 %collective-permute-start.1 = (bf16[128,1536]{1,0:T(8,128)(2,1)S(1)}, bf16[128,1536]{1,0:T(8,128)(2,1)S(1)}, u32[]{:S(2)}, u32[]{:S(2)}) collective-permute-start(bf16[128,1536]{1,0:T(8,128)(2,1)S(1)} %shard_map.81), channel_id=1, source_target_pairs={{0,2},{2,4},{4,6},{6,0},{1,3},{3,5},{5,7},{7,1},{8,10},{10,12},{12... | collective-permute-start | bytes 1179656 | tf_op jit(solution)/shard_map/ppermute | solution.py:162
  119.9 16.5 %collective-permute-start.2 = (bf16[128,1536]{1,0:T(8,128)(2,1)S(1)}, bf16[128,1536]{1,0:T(8,128)(2,1)S(1)}, u32[]{:S(2)}, u32[]{:S(2)}) collective-permute-start(bf16[128,1536]{1,0:T(8,128)(2,1)S(1)} %shard_map.82), channel_id=1, source_target_pairs={{0,6},{2,0},{4,2},{6,4},{1,7},{3,1},{5,3},{7,5},{8,14},{10,8},{12,... | collective-permute-start | bytes 1179656 | tf_op jit(solution)/shard_map/ppermute | solution.py:162

commit v5 on v4

--- a/solution.py
+++ b/solution.py
@@ -6,12 +6,11 @@
 from jax.sharding import Mesh
 from jax.sharding import PartitionSpec as P
 
-EMPTY = 8.0
-DIGIT = 64
 NEAR = 2
 SLOTS = 2
-BLOCK = NEAR * 2
-LANES = 128
+CORES = 2
+BLOCK = NEAR * CORES
+SUBLANES = 8
 
 f32, bf16 = jnp.float32, jnp.bfloat16
 WHOLE = pl.BlockSpec(memory_space=pltpu.VMEM)
@@ -59,15 +58,16 @@
     half = lanes // SLOTS
     out_ref[:, width:] = placed(ids[...], lanes, lane % half, lane // half).astype(bf16)
     slot = lane // SLOTS
-    far = half // BLOCK
-    mix = placed(ids[...], lanes, slot % far * BLOCK + slot // far, lane % SLOTS, weights[...])
+    chip = slot % (half // CORES)
+    expert = chip // NEAR * BLOCK + chip % NEAR * CORES + slot // (half // CORES)
+    mix = placed(ids[...], lanes, expert, lane % SLOTS, weights[...])
     high = mix.astype(bf16)
     high_ref[...] = high
     low_ref[...] = (mix - high.astype(f32)).astype(bf16)
     token_copy.wait()
 
 
-def select_kernel(block_ref, gathered_ref, out_ref):
+def select_kernel(block_ref, gathered_ref, out_ref, loads_ref):
     copies, count, width = out_ref.shape
     lanes = gathered_ref.shape[1] - width
     tokens = gathered_ref.shape[0]
@@ -75,7 +75,8 @@
     far = count // (SLOTS * BLOCK)
     row = iota((lanes, count), 1)
     lane = iota((lanes, count), 0)
-    expert = block_ref[0] * BLOCK + row // (far * SLOTS)
+    device = row // (far * SLOTS)
+    expert = block_ref[0] * BLOCK + device % NEAR * CORES + device // NEAR
     pick = jnp.where(lane == row % SLOTS * experts + expert, 1.0, 0.0).astype(bf16)
     chosen = jnp.dot(gathered_ref[:, width:], pick, preferred_element_type=f32)
     source = iota((tokens, count), 0) // (tokens // far)
@@ -83,15 +84,13 @@
     chosen = jnp.where(mine, chosen, 0.0).astype(bf16)
     contract = (((0,), (0,)), ((), ()))
     rows = lax.dot_general(chosen, gathered_ref[:, :width], contract, preferred_element_type=f32)
-    held = lax.dot_general(
-        chosen, jnp.ones((tokens, LANES), bf16), contract, preferred_element_type=f32
-    )
-    empty = (held < 0.5) & (iota((count, LANES), 1) == 0)
-    start = jnp.where(empty, EMPTY, rows[:, :LANES]).astype(bf16)
-    rest = rows[:, LANES:].astype(bf16)
     for copy in range(copies):
-        out_ref[copy, :, :LANES] = start
-        out_ref[copy, :, LANES:] = rest
+        out_ref[copy] = rows.astype(bf16)
+    loads_ref[...] = jnp.dot(
+        jnp.ones((loads_ref.shape[0], tokens), bf16),
+        gathered_ref[:, width:],
+        preferred_element_type=f32,
+    )
 
 
 def expert_kernel(peer_ref, rows_ref, gate_ref, up_ref, down_ref, out_ref):
@@ -122,35 +121,19 @@
     )(peer, rows, gate_part, up_part, down_part)
 
 
-def finish_kernel(rows_ref, own_ref, *refs):
+def finish_kernel(own_ref, *refs):
     *terms, out_ref = refs
     total = own_ref[...]
     for term_ref in terms:
         total = total + term_ref[...].astype(f32)
-    width = total.shape[1]
-    out_ref[:, :width] = total.astype(bf16)
-    held = jnp.where(rows_ref[:, :LANES].astype(f32) < EMPTY - 1, 1.0, 0.0)
-    load = jnp.sum(held, axis=0, keepdims=True)[:, :1]
-    high = jnp.floor(load / DIGIT)
-    lane = iota((total.shape[0], LANES), 1)
-    out_ref[:, width:] = jnp.where(lane == 0, high, load - high * DIGIT).astype(bf16)
-
-
-def mix_kernel(returned_ref, high_ref, low_ref, mixed_ref, loads_ref):
-    width = mixed_ref.shape[1]
-    count = returned_ref.shape[0]
-    far = count // (SLOTS * BLOCK)
-    rows = returned_ref[:, :width]
+    out_ref[...] = total.astype(bf16)
+
+
+def mix_kernel(returned_ref, high_ref, low_ref, mixed_ref):
+    rows = returned_ref[...]
     mixed = jnp.dot(high_ref[...], rows, preferred_element_type=f32)
     mixed = mixed + jnp.dot(low_ref[...], rows, preferred_element_type=f32)
     mixed_ref[...] = mixed.astype(bf16)
-    digits = returned_ref[:, width : width + LANES].astype(f32)
-    load = digits[:, :1] * DIGIT + digits[:, 1:2]
-    shape = (count, LANES)
-    expert = iota(shape, 1)
-    first = (expert % BLOCK * far + expert // BLOCK) * SLOTS
-    load = jnp.where(iota(shape, 0) == first, load, 0.0)
-    loads_ref[...] = jnp.sum(load, axis=0, keepdims=True).astype(jnp.int32)
 
 
 def all_to_all(array, axis):
@@ -190,15 +173,18 @@
     peers = [((me + step) % tp).reshape(1) for step in steps]
     packed, block, *peers = lax.optimization_barrier((packed, block, *peers))
     gathered = lax.all_gather(packed, "eh", tiled=True)
-    outgoing = pl.pallas_call(
+    outgoing, loads = pl.pallas_call(
         select_kernel,
-        out_shape=jax.ShapeDtypeStruct((tp, slots, width), bf16),
+        out_shape=(
+            jax.ShapeDtypeStruct((tp, slots, width), bf16),
+            jax.ShapeDtypeStruct((SUBLANES, slots), f32),
+        ),
         in_specs=[pl.BlockSpec(memory_space=pltpu.SMEM), WHOLE],
-        out_specs=WHOLE,
+        out_specs=(WHOLE, WHOLE),
         compiler_params=PARAMS,
     )(block, gathered)
-    outgoing = outgoing.reshape(tp * near * dp, far * SLOTS, width)
-    arrived = all_to_all(outgoing, ("tp", "el", "dp")).reshape(tp * slots, width)
+    outgoing = outgoing.reshape(tp * dp * near, far * SLOTS, width)
+    arrived = all_to_all(outgoing, ("tp", "dp", "el")).reshape(tp * slots, width)
 
     terms = []
     for turn, step in enumerate(steps[:-1]):
@@ -207,23 +193,30 @@
     own = expert_apply(peers[-1], arrived, w_gate, w_up, w_down, slots, f32)
     finished = pl.pallas_call(
         finish_kernel,
-        out_shape=jax.ShapeDtypeStruct((slots, width + LANES), bf16),
-        in_specs=[WHOLE] * (2 + len(terms)),
+        out_shape=jax.ShapeDtypeStruct((slots, width), bf16),
+        in_specs=[WHOLE] * (1 + len(terms)),
         out_specs=WHOLE,
         compiler_params=PARAMS,
-    )(arrived, own, *terms)
-    returned = all_to_all(finished.reshape(experts, SLOTS, -1), ("el", "dp", "eh"))
-    mixed, loads = pl.pallas_call(
+    )(own, *terms)
+    finished = finished.reshape(dp, near, far, SLOTS, width).swapaxes(1, 2)
+    returned = all_to_all(finished.reshape(experts, SLOTS, width), ("dp", "eh", "el"))
+
+    turn = 0
+    for axis in ("el", "dp", "tp"):
+        step = 1
+        while step < lax.axis_size(axis):
+            other = shifted(loads, axis, step)
+            loads = loads + other
+            step, turn = 2 * step, turn + 1
+    mixed = pl.pallas_call(
         mix_kernel,
-        out_shape=(
-            jax.ShapeDtypeStruct((count, width), bf16),
-            jax.ShapeDtypeStruct((1, LANES), jnp.int32),
-        ),
+        out_shape=jax.ShapeDtypeStruct((count, width), bf16),
         in_specs=[WHOLE] * 3,
-        out_specs=(WHOLE, WHOLE),
-        compiler_params=PARAMS,
-    )(returned.reshape(slots, -1), high, low)
-    return mixed, loads[0, :experts]
+        out_specs=WHOLE,
+        compiler_params=PARAMS,
+    )(returned.reshape(slots, width), high, low)
+    loads = loads[0, :experts] + loads[0, experts:]
+    return mixed, loads.astype(jnp.int32)
 
 
 def solution(mesh):

time: 205 us -> 201 us (0.980)
  blocking collectives: 171 us -> 107 us
  waiting for transfers between devices: 11.2 us -> 48.1 us
  starting transfers between devices: 9.93 us -> 31.9 us
    all_to_all x2 -> x1, blocking collectives: 89.8 us -> 25.7 us  [all_to_all(): return lax.all_to_all(array, axis, split_axis=0, concat_axis=0, tiled=True)]
    ppermute x3 -> x7, waiting for transfers between devices: 11.2 us -> 48.1 us  [shifted(): lax.ppermute(array, axis, [(i, (i + step) % size) for i in range(size)])]
    all_to_all x0 -> x1, starting transfers between devices: none -> 11.3 us  [all_to_all(): return lax.all_to_all(array, axis, split_axis=0, concat_axis=0, tiled=True)]
    ppermute x3 -> x7, starting transfers between devices: 9.93 us -> 20.6 us  [shifted(): lax.ppermute(array, axis, [(i, (i + step) % size) for i in range(size)])]
  transfers between devices with their start and end apart: 3 -> 8, of which waited for: 2 -> 6; matrix products, arithmetic and copies ran while one was open for 0% -> 0% of each run, Pallas kernels for 0% -> 0%
where the time goes in v5:
time: 201 us; the launch traced here: 197 us
  blocking collectives  107 us (53%)
  waiting for transfers between devices  48.1 us (24%)
  starting transfers between devices  31.9 us (16%)
  Pallas kernels  5.71 us (3%)
  local copies, waits for them, and re-layouts  3.5 us (2%)
    all_gather x1, blocking collectives, per_device(): gathered = lax.all_gather(packed, 'eh', tiled=True)  81 us
    ppermute x7, waiting for transfers between devices, shifted(): lax.ppermute(array, axis, [(i, (i + step) % size) for i in range(size)])  48.1 us
    all_to_all x1, blocking collectives, all_to_all(): return lax.all_to_all(array, axis, split_axis=0, concat_axis=0, tiled=True)  25.7 us
    ppermute x7, starting transfers between devices, shifted(): lax.ppermute(array, axis, [(i, (i + step) % size) for i in range(size)])  20.6 us
    all_to_all x1, starting transfers between devices, all_to_all(): return lax.all_to_all(array, axis, split_axis=0, concat_axis=0, tiled=True)  11.3 us
  transfers between devices with their start and end apart: 8, of which 6 were waited for; matrix products, arithmetic and copies ran while one was open for 0% of the time, Pallas kernels for 0%

profile of v5, /device:TPU:40, one launch (start us, length us, event | category | flops | bytes accessed | tf_op | source)
XLA Modules:
  0.0 197.4 jit_solution(5921888669508022749)
XLA Ops:
  0.7 0.0 copy-start.3
  0.7 0.8 copy-done.3
  1.5 0.0 copy-start.4
  1.5 0.7 copy-done.4
  2.2 0.0 copy-start.5
  2.2 0.7 copy-done.5
  2.8 0.3 shard_map.77
  3.1 81.0 %all_gather.3.gathered_ref = bf16[256,1664]{1,0:T(8,128)(2,1)S(1)} all-gather(bf16[16,1664]{1,0:T(8,128)(2,1)S(1)} %get-tuple-element.16), channel_id=1, replica_groups=mesh['groups'=2,'eh'=16,'el'=2,'tp'=4,'dp'=2] {'eh'}, dimensions={0}, use_global_device_ids=true | all-gather | bytes 905216 | tf_op jit(solution)/shard_map/all_gather | solution.py:175
  84.1 0.0 copy-start.2
  84.1 0.5 shard_map.78
  84.6 0.0 copy-start
  84.6 0.0 copy-start.1
  84.6 25.7 %all_to_all.10 = bf16[16,32,1536]{2,1,0:T(8,128)(2,1)S(1)} all-to-all(bf16[16,32,1536]{2,1,0:T(8,128)(2,1)S(1)} %bitcast.17), channel_id=1, replica_groups=mesh['groups'=2,'eh'=16,'el'=2,'tp'=4,'dp'=2] {'tp','dp','el'}, dimensions={0} | all-to-all | bytes 3145728 | tf_op jit(solution)/shard_map/all_to_all | solution.py:140
  110.3 0.0 copy-done.2
  110.3 0.0 copy-done
  110.3 0.0 copy-done.1
  110.3 1.0 shard_map.82
  111.3 1.0 shard_map.81
  112.3 1.0 shard_map.80
  113.3 3.8 %collective-permute-start = (bf16[128,1536]{1,0:T(8,128)(2,1)S(1)}, bf16[128,1536]{1,0:T(8,128)(2,1)S(1)}, u32[]{:S(2)}, u32[]{:S(2)}) collective-permute-start(bf16[128,1536]{1,0:T(8,128)(2,1)S(1)} %shard_map.80), channel_id=1, source_target_pairs={{0,4},{2,6},{4,0},{6,2},{1,5},{3,7},{5,1},{7,3},{8,12},{10,14},{12... | collective-permute-start | bytes 1179656 | tf_op jit(solution)/shard_map/ppermute | solution.py:145
  117.1 2.5 %collective-permute-start.1 = (bf16[128,1536]{1,0:T(8,128)(2,1)S(1)}, bf16[128,1536]{1,0:T(8,128)(2,1)S(1)}, u32[]{:S(2)}, u32[]{:S(2)}) collective-permute-start(bf16[128,1536]{1,0:T(8,128)(2,1)S(1)} %shard_map.81), channel_id=1, source_target_pairs={{0,2},{2,4},{4,6},{6,0},{1,3},{3,5},{5,7},{7,1},{8,10},{10,12},{12... | collective-permute-start | bytes 1179656 | tf_op jit(solution)/shard_map/ppermute | solution.py:145
  119.7 4.6 %collective-permute-start.2 = (bf16[128,1536]{1,0:T(8,128)(2,1)S(1)}, bf16[128,1536]{1,0:T(8,128)(2,1)S(1)}, u32[]{:S(2)}, u32[]{:S(2)}) collective-permute-start(bf16[128,1536]{1,0:T(8,128)(2,1)S(1)} %shard_map.82), channel_id=1, source_target_pairs={{0,6},{2,0},{4,2},{6,4},{1,7},{3,1},{5,3},{7,5},{8,14},{10,8},{12,... | collective-permute-start | bytes 1179656 | tf_op jit(solution)/shard_map/ppermute | solution.py:145
  124.3 1.0 shard_map.79.own_ref
  125.3 3.5 %collective-permute-done.refs_0_ = bf16[128,1536]{1,0:T(8,128)(2,1)S(1)} collective-permute-done((bf16[128,1536]{1,0:T(8,128)(2,1)S(1)}, bf16[128,1536]{1,0:T(8,128)(2,1)S(1)}, u32[]{:S(2)}, u32[]{:S(2)}) %collective-permute-start) | collective-permute-done | bytes 393248 | tf_op jit(solution)/shard_map/ppermute | solution.py:145
  128.8 7.6 %collective-permute-done.1.refs_1_ = bf16[128,1536]{1,0:T(8,128)(2,1)S(1)} collective-permute-done((bf16[128,1536]{1,0:T(8,128)(2,1)S(1)}, bf16[128,1536]{1,0:T(8,128)(2,1)S(1)}, u32[]{:S(2)}, u32[]{:S(2)}) %collective-permute-start.1) | collective-permute-done | bytes 393248 | tf_op jit(solution)/shard_map/ppermute | solution.py:145
  136.3 0.0 collective-permute-done.2.refs_2_
  136.3 0.2 shard_map.83
  136.5 0.1 reshape.43
  136.7 1.0 copy.8
  137.7 11.3 %all-to-all-start.1 = ((bf16[64,2,1536]{2,1,0:T(2,128)(2,1)}), bf16[64,2,1536]{2,1,0:T(2,128)(2,1)S(1)}, u32[]{:S(2)}, u32[]{:S(2)}) async-start(bf16[64,2,1536]{2,1,0:T(2,128)(2,1)} %bitcast.10), calls=%async_computation.1 | async-start | bytes 786432 | tf_op jit(solution)/shard_map/all_to_all | solution.py:140
  149.0 2.6 %collective-permute-start.3 = (f32[8,128]{1,0:T(8,128)S(1)}, f32[8,128]{1,0:T(8,128)S(1)}, u32[]{:S(2)}, u32[]{:S(2)}) collective-permute-start(f32[8,128]{1,0:T(8,128)S(1)} %get-tuple-element.23), channel_id=1, source_target_pairs={{0,8},{8,0},{1,9},{9,1},{2,10},{10,2},{3,11},{11,3},{4,12},{12,4},... | collective-permute-start | bytes 12296 | tf_op jit(solution)/shard_map/ppermute | solution.py:145
  151.7 27.2 %collective-permute-done.3 = f32[8,128]{1,0:T(8,128)S(1)} collective-permute-done((f32[8,128]{1,0:T(8,128)S(1)}, f32[8,128]{1,0:T(8,128)S(1)}, u32[]{:S(2)}, u32[]{:S(2)}) %collective-permute-start.3) | collective-permute-done | bytes 4128 | tf_op jit(solution)/shard_map/ppermute | solution.py:145
  178.9 1.9 collective-permute-start.4
  180.9 1.1 collective-permute-done.4
  182.0 2.5 %collective-permute-start.5 = (f32[8,128]{1,0:T(8,128)S(1)}, f32[8,128]{1,0:T(8,128)S(1)}, u32[]{:S(2)}, u32[]{:S(2)}) collective-permute-start(f32[8,128]{1,0:T(8,128)S(1)} %add.46), channel_id=1, source_target_pairs={{0,2},{2,4},{4,6},{6,0},{1,3},{3,5},{5,7},{7,1},{8,10},{10,12},{12... | collective-permute-start | bytes 12296 | tf_op jit(solution)/shard_map/ppermute | solution.py:145
  184.5 4.2 %collective-permute-done.5 = f32[8,128]{1,0:T(8,128)S(1)} collective-permute-done((f32[8,128]{1,0:T(8,128)S(1)}, f32[8,128]{1,0:T(8,128)S(1)}, u32[]{:S(2)}, u32[]{:S(2)}) %collective-permute-start.5) | collective-permute-done | bytes 4128 | tf_op jit(solution)/shard_map/ppermute | solution.py:145
  188.8 2.5 %collective-permute-start.6 = (f32[8,128]{1,0:T(8,128)S(1)}, f32[8,128]{1,0:T(8,128)S(1)}, u32[]{:S(2)}, u32[]{:S(2)}) collective-permute-start(f32[8,128]{1,0:T(8,128)S(1)} %add.47), channel_id=1, source_target_pairs={{0,4},{2,6},{4,0},{6,2},{1,5},{3,7},{5,1},{7,3},{8,12},{10,14},{12... | collective-permute-start | bytes 12296 | tf_op jit(solution)/shard_map/ppermute | solution.py:145
  191.3 4.5 %collective-permute-done.6 = f32[8,128]{1,0:T(8,128)S(1)} collective-permute-done((f32[8,128]{1,0:T(8,128)S(1)}, f32[8,128]{1,0:T(8,128)S(1)}, u32[]{:S(2)}, u32[]{:S(2)}) %collective-permute-start.6) | collective-permute-done | bytes 4128 | tf_op jit(solution)/shard_map/ppermute | solution.py:145
  195.8 0.6 convert_bitcast_fusion
  196.4 0.0 all-to-all-done.1
  196.4 0.1 reshape.45.returned_ref
  196.5 0.8 shard_map.84
  (4 shorter events, 0.0 us)
Async XLA Ops:
  0.7 0.8 copy-start.3
  1.5 0.7 copy-start.4
  2.2 0.7 copy-start.5
  84.1 26.2 %copy-start.2 = (bf16[1,1536,384]{2,1,0:T(8,128)(2,1)S(1)}, bf16[1,1536,384]{2,1,0:T(8,128)(2,1)}, u32[]{:S(2)}) copy-start(bf16[1,1536,384]{2,1,0:T(8,128)(2,1)} %down_ref.7) | copy-start | bytes 3538948
  84.6 25.8 %copy-start = (bf16[1,1536,384]{2,1,0:T(8,128)(2,1)S(1)}, bf16[1,1536,384]{2,1,0:T(8,128)(2,1)}, u32[]{:S(2)}) copy-start(bf16[1,1536,384]{2,1,0:T(8,128)(2,1)} %gate_ref.7) | copy-start | bytes 3538948
  84.6 25.7 %copy-start.1 = (bf16[1,1536,384]{2,1,0:T(8,128)(2,1)S(1)}, bf16[1,1536,384]{2,1,0:T(8,128)(2,1)}, u32[]{:S(2)}) copy-start(bf16[1,1536,384]{2,1,0:T(8,128)(2,1)} %up_ref.7) | copy-start | bytes 3538948
  113.3 15.5 %collective-permute-start = (bf16[128,1536]{1,0:T(8,128)(2,1)S(1)}, bf16[128,1536]{1,0:T(8,128)(2,1)S(1)}, u32[]{:S(2)}, u32[]{:S(2)}) collective-permute-start(bf16[128,1536]{1,0:T(8,128)(2,1)S(1)} %shard_map.80), channel_id=1, source_target_pairs={{0,4},{2,6},{4,0},{6,2},{1,5},{3,7},{5,1},{7,3},{8,12},{10,14},{12... | collective-permute-start | bytes 1179656 | tf_op jit(solution)/shard_map/ppermute | solution.py:145
  117.1 19.2 %collective-permute-start.1 = (bf16[128,1536]{1,0:T(8,128)(2,1)S(1)}, bf16[128,1536]{1,0:T(8,128)(2,1)S(1)}, u32[]{:S(2)}, u32[]{:S(2)}) collective-permute-start(bf16[128,1536]{1,0:T(8,128)(2,1)S(1)} %shard_map.81), channel_id=1, source_target_pairs={{0,2},{2,4},{4,6},{6,0},{1,3},{3,5},{5,7},{7,1},{8,10},{10,12},{12... | collective-permute-start | bytes 1179656 | tf_op jit(solution)/shard_map/ppermute | solution.py:145
  119.7 16.7 %collective-permute-start.2 = (bf16[128,1536]{1,0:T(8,128)(2,1)S(1)}, bf16[128,1536]{1,0:T(8,128)(2,1)S(1)}, u32[]{:S(2)}, u32[]{:S(2)}) collective-permute-start(bf16[128,1536]{1,0:T(8,128)(2,1)S(1)} %shard_map.82), channel_id=1, source_target_pairs={{0,6},{2,0},{4,2},{6,4},{1,7},{3,1},{5,3},{7,5},{8,14},{10,8},{12,... | collective-permute-start | bytes 1179656 | tf_op jit(solution)/shard_map/ppermute | solution.py:145
  137.7 58.7 %all-to-all-start.1 = ((bf16[64,2,1536]{2,1,0:T(2,128)(2,1)}), bf16[64,2,1536]{2,1,0:T(2,128)(2,1)S(1)}, u32[]{:S(2)}, u32[]{:S(2)}) async-start(bf16[64,2,1536]{2,1,0:T(2,128)(2,1)} %bitcast.10), calls=%async_computation.1 | async-start | bytes 786432 | tf_op jit(solution)/shard_map/all_to_all | solution.py:140
  149.0 29.9 %collective-permute-start.3 = (f32[8,128]{1,0:T(8,128)S(1)}, f32[8,128]{1,0:T(8,128)S(1)}, u32[]{:S(2)}, u32[]{:S(2)}) collective-permute-start(f32[8,128]{1,0:T(8,128)S(1)} %get-tuple-element.23), channel_id=1, source_target_pairs={{0,8},{8,0},{1,9},{9,1},{2,10},{10,2},{3,11},{11,3},{4,12},{12,4},... | collective-permute-start | bytes 12296 | tf_op jit(solution)/shard_map/ppermute | solution.py:145
  178.9 3.1 %collective-permute-start.4 = (f32[8,128]{1,0:T(8,128)S(1)}, f32[8,128]{1,0:T(8,128)S(1)}, u32[]{:S(2)}, u32[]{:S(2)}) collective-permute-start(f32[8,128]{1,0:T(8,128)S(1)} %add.45), channel_id=1, source_target_pairs={{0,1},{1,0},{2,3},{3,2},{4,5},{5,4},{6,7},{7,6},{8,9},{9,8},{10,11... | collective-permute-start | bytes 12296 | tf_op jit(solution)/shard_map/ppermute | solution.py:145
  182.0 6.7 %collective-permute-start.5 = (f32[8,128]{1,0:T(8,128)S(1)}, f32[8,128]{1,0:T(8,128)S(1)}, u32[]{:S(2)}, u32[]{:S(2)}) collective-permute-start(f32[8,128]{1,0:T(8,128)S(1)} %add.46), channel_id=1, source_target_pairs={{0,2},{2,4},{4,6},{6,0},{1,3},{3,5},{5,7},{7,1},{8,10},{10,12},{12... | collective-permute-start | bytes 12296 | tf_op jit(solution)/shard_map/ppermute | solution.py:145
  188.8 7.0 %collective-permute-start.6 = (f32[8,128]{1,0:T(8,128)S(1)}, f32[8,128]{1,0:T(8,128)S(1)}, u32[]{:S(2)}, u32[]{:S(2)}) collective-permute-start(f32[8,128]{1,0:T(8,128)S(1)} %add.47), channel_id=1, source_target_pairs={{0,4},{2,6},{4,0},{6,2},{1,5},{3,7},{5,1},{7,3},{8,12},{10,14},{12... | collective-permute-start | bytes 12296 | tf_op jit(solution)/shard_map/ppermute | solution.py:145

commit v6 on v5

--- a/solution.py
+++ b/solution.py
@@ -41,30 +41,26 @@
     return jnp.where(chosen, named if values is None else value, 0.0)
 
 
-def pack_kernel(
-    tokens_ref, ids_ref, weights_ref, out_ref, high_ref, low_ref, ids, weights, token_sem, ids_sem, weights_sem
-):
-    count, width = tokens_ref.shape
+def pack_kernel(tokens_ref, ids_ref, out_ref):
+    width = tokens_ref.shape[1]
     lanes = out_ref.shape[1] - width
-    token_copy = pltpu.make_async_copy(tokens_ref, out_ref.at[:, pl.ds(0, width)], token_sem)
-    ids_copy = pltpu.make_async_copy(ids_ref, ids, ids_sem)
-    weights_copy = pltpu.make_async_copy(weights_ref, weights, weights_sem)
-    ids_copy.start()
-    weights_copy.start()
-    token_copy.start()
-    ids_copy.wait()
-    weights_copy.wait()
-    lane = iota((count, lanes), 1)
+    lane = iota((tokens_ref.shape[0], lanes), 1)
     half = lanes // SLOTS
-    out_ref[:, width:] = placed(ids[...], lanes, lane % half, lane // half).astype(bf16)
+    out_ref[:, :width] = tokens_ref[...]
+    out_ref[:, width:] = placed(ids_ref[...], lanes, lane % half, lane // half).astype(bf16)
+
+
+def gates_kernel(ids_ref, weights_ref, high_ref, low_ref):
+    lanes = high_ref.shape[1]
+    lane = iota(high_ref.shape, 1)
+    half = lanes // SLOTS
     slot = lane // SLOTS
     chip = slot % (half // CORES)
     expert = chip // NEAR * BLOCK + chip % NEAR * CORES + slot // (half // CORES)
-    mix = placed(ids[...], lanes, expert, lane % SLOTS, weights[...])
+    mix = placed(ids_ref[...], lanes, expert, lane % SLOTS, weights_ref[...])
     high = mix.astype(bf16)
     high_ref[...] = high
     low_ref[...] = (mix - high.astype(f32)).astype(bf16)
-    token_copy.wait()
 
 
 def select_kernel(block_ref, gathered_ref, out_ref, loads_ref):
@@ -152,22 +148,13 @@
     experts = far * near * dp
     slots = experts * SLOTS
     steps = (*range(2, tp - 1), 1, tp - 1, 0)
-    packed, high, low = pl.pallas_call(
+    packed = pl.pallas_call(
         pack_kernel,
-        out_shape=(
-            jax.ShapeDtypeStruct((count, width + slots), bf16),
-            jax.ShapeDtypeStruct((count, slots), bf16),
-            jax.ShapeDtypeStruct((count, slots), bf16),
-        ),
-        in_specs=[pl.BlockSpec(memory_space=pl.ANY)] * 3,
-        out_specs=(WHOLE,) * 3,
-        scratch_shapes=[
-            pltpu.VMEM((expert_ids.shape[1], count), jnp.int32),
-            pltpu.VMEM((expert_ids.shape[1], count), f32),
-            *[pltpu.SemaphoreType.DMA] * 3,
-        ],
-        compiler_params=PARAMS,
-    )(tokens, expert_ids.T, gate_weights.T)
+        out_shape=jax.ShapeDtypeStruct((count, width + slots), bf16),
+        in_specs=[WHOLE] * 2,
+        out_specs=WHOLE,
+        compiler_params=PARAMS,
+    )(tokens, expert_ids.T)
     me = lax.axis_index("tp").astype(jnp.int32)
     block = lax.axis_index("eh").astype(jnp.int32).reshape(1)
     peers = [((me + step) % tp).reshape(1) for step in steps]
@@ -208,6 +195,13 @@
             other = shifted(loads, axis, step)
             loads = loads + other
             step, turn = 2 * step, turn + 1
+    high, low = pl.pallas_call(
+        gates_kernel,
+        out_shape=(jax.ShapeDtypeStruct((count, slots), bf16),) * 2,
+        in_specs=[WHOLE] * 2,
+        out_specs=(WHOLE, WHOLE),
+        compiler_params=PARAMS,
+    )(expert_ids.T, gate_weights.T)
     mixed = pl.pallas_call(
         mix_kernel,
         out_shape=jax.ShapeDtypeStruct((count, width), bf16),

time: 201 us -> 199 us (0.990)
  the two profiles are of different devices: /device:TPU:40 before, /device:TPU:33 now
where the time goes in v6:
time: 199 us; the launch traced here: 198 us
  blocking collectives  108 us (54%)
  waiting for transfers between devices  45.1 us (23%)
  starting transfers between devices  35.1 us (18%)
  Pallas kernels  5.9 us (3%)
  local copies, waits for them, and re-layouts  2.82 us (1%)
    all_gather x1, blocking collectives, per_device(): gathered = lax.all_gather(packed, 'eh', tiled=True)  74.8 us
    ppermute x7, waiting for transfers between devices, shifted(): lax.ppermute(array, axis, [(i, (i + step) % size) for i in range(size)])  44.6 us
    all_to_all x1, blocking collectives, all_to_all(): return lax.all_to_all(array, axis, split_axis=0, concat_axis=0, tiled=True)  33 us
    ppermute x7, starting transfers between devices, shifted(): lax.ppermute(array, axis, [(i, (i + step) % size) for i in range(size)])  20.7 us
    all_to_all x1, starting transfers between devices, all_to_all(): return lax.all_to_all(array, axis, split_axis=0, concat_axis=0, tiled=True)  14.3 us
  transfers between devices with their start and end apart: 8, of which 7 were waited for; matrix products, arithmetic and copies ran while one was open for 0% of the time, Pallas kernels for 2%

profile of v6, /device:TPU:33, one launch (start us, length us, event | category | flops | bytes accessed | tf_op | source)
XLA Modules:
  0.0 198.1 jit_solution(13017991599210543154)
XLA Ops:
  0.7 0.0 copy-start.3
  0.7 0.8 copy-done.3
  1.5 0.0 copy-start.4
  1.5 0.7 copy-done.4
  2.2 0.2 shard_map.77
  2.4 74.8 %all_gather.3.gathered_ref = bf16[256,1664]{1,0:T(8,128)(2,1)S(1)} all-gather(bf16[16,1664]{1,0:T(8,128)(2,1)S(1)} %shard_map.77), channel_id=1, replica_groups=mesh['groups'=2,'eh'=16,'el'=2,'tp'=4,'dp'=2] {'eh'}, dimensions={0}, use_global_device_ids=true | all-gather | bytes 905216 | tf_op jit(solution)/shard_map/all_gather | solution.py:162
  77.2 0.0 copy-start.2
  77.2 0.5 shard_map.78
  77.6 0.0 copy-start
  77.6 0.0 copy-start.1
  77.7 33.0 %all_to_all.10 = bf16[16,32,1536]{2,1,0:T(8,128)(2,1)S(1)} all-to-all(bf16[16,32,1536]{2,1,0:T(8,128)(2,1)S(1)} %bitcast.17), channel_id=1, replica_groups=mesh['groups'=2,'eh'=16,'el'=2,'tp'=4,'dp'=2] {'tp','dp','el'}, dimensions={0} | all-to-all | bytes 3145728 | tf_op jit(solution)/shard_map/all_to_all | solution.py:136
  110.6 0.0 copy-done.2
  110.6 0.0 copy-done
  110.6 0.0 copy-done.1
  110.6 1.0 shard_map.80
  111.6 3.5 %collective-permute-start = (bf16[128,1536]{1,0:T(8,128)(2,1)S(1)}, bf16[128,1536]{1,0:T(8,128)(2,1)S(1)}, u32[]{:S(2)}, u32[]{:S(2)}) collective-permute-start(bf16[128,1536]{1,0:T(8,128)(2,1)S(1)} %shard_map.80), channel_id=1, source_target_pairs={{0,4},{2,6},{4,0},{6,2},{1,5},{3,7},{5,1},{7,3},{8,12},{10,14},{12... | collective-permute-start | bytes 1179656 | tf_op jit(solution)/shard_map/ppermute | solution.py:141
  115.1 1.0 shard_map.81
  116.1 2.0 collective-permute-start.1
  118.1 1.0 shard_map.82
  119.1 4.6 %collective-permute-start.2 = (bf16[128,1536]{1,0:T(8,128)(2,1)S(1)}, bf16[128,1536]{1,0:T(8,128)(2,1)S(1)}, u32[]{:S(2)}, u32[]{:S(2)}) collective-permute-start(bf16[128,1536]{1,0:T(8,128)(2,1)S(1)} %shard_map.82), channel_id=1, source_target_pairs={{0,6},{2,0},{4,2},{6,4},{1,7},{3,1},{5,3},{7,5},{8,14},{10,8},{12,... | collective-permute-start | bytes 1179656 | tf_op jit(solution)/shard_map/ppermute | solution.py:141
  123.7 1.0 shard_map.79.own_ref
  124.7 0.8 collective-permute-done.refs_0_
  125.4 9.1 %collective-permute-done.1.refs_1_ = bf16[128,1536]{1,0:T(8,128)(2,1)S(1)} collective-permute-done((bf16[128,1536]{1,0:T(8,128)(2,1)S(1)}, bf16[128,1536]{1,0:T(8,128)(2,1)S(1)}, u32[]{:S(2)}, u32[]{:S(2)}) %collective-permute-start.1) | collective-permute-done | bytes 393248 | tf_op jit(solution)/shard_map/ppermute | solution.py:141
  134.5 0.0 collective-permute-done.2.refs_2_
  134.5 0.2 shard_map.83
  134.7 0.0 copy-start.5
  134.7 0.0 copy-start.6
  134.8 0.1 reshape.43
  134.9 1.0 copy.8
  135.9 14.3 %all-to-all-start.1 = ((bf16[64,2,1536]{2,1,0:T(2,128)(2,1)}), bf16[64,2,1536]{2,1,0:T(2,128)(2,1)S(1)}, u32[]{:S(2)}, u32[]{:S(2)}) async-start(bf16[64,2,1536]{2,1,0:T(2,128)(2,1)} %bitcast.9), calls=%async_computation.1 | async-start | bytes 786432 | tf_op jit(solution)/shard_map/all_to_all | solution.py:136
  150.3 3.3 %collective-permute-start.3 = (f32[8,128]{1,0:T(8,128)S(1)}, f32[8,128]{1,0:T(8,128)S(1)}, u32[]{:S(2)}, u32[]{:S(2)}) collective-permute-start(f32[8,128]{1,0:T(8,128)S(1)} %get-tuple-element.21), channel_id=1, source_target_pairs={{0,8},{8,0},{1,9},{9,1},{2,10},{10,2},{3,11},{11,3},{4,12},{12,4},... | collective-permute-start | bytes 12296 | tf_op jit(solution)/shard_map/ppermute | solution.py:141
  153.6 26.6 %collective-permute-done.3 = f32[8,128]{1,0:T(8,128)S(1)} collective-permute-done((f32[8,128]{1,0:T(8,128)S(1)}, f32[8,128]{1,0:T(8,128)S(1)}, u32[]{:S(2)}, u32[]{:S(2)}) %collective-permute-start.3) | collective-permute-done | bytes 4128 | tf_op jit(solution)/shard_map/ppermute | solution.py:141
  180.2 2.9 %collective-permute-start.4 = (f32[8,128]{1,0:T(8,128)S(1)}, f32[8,128]{1,0:T(8,128)S(1)}, u32[]{:S(2)}, u32[]{:S(2)}) collective-permute-start(f32[8,128]{1,0:T(8,128)S(1)} %add.45), channel_id=1, source_target_pairs={{0,1},{1,0},{2,3},{3,2},{4,5},{5,4},{6,7},{7,6},{8,9},{9,8},{10,11... | collective-permute-start | bytes 12296 | tf_op jit(solution)/shard_map/ppermute | solution.py:141
  183.2 0.8 collective-permute-done.4
  184.0 2.2 %collective-permute-start.5 = (f32[8,128]{1,0:T(8,128)S(1)}, f32[8,128]{1,0:T(8,128)S(1)}, u32[]{:S(2)}, u32[]{:S(2)}) collective-permute-start(f32[8,128]{1,0:T(8,128)S(1)} %add.46), channel_id=1, source_target_pairs={{0,2},{2,4},{4,6},{6,0},{1,3},{3,5},{5,7},{7,1},{8,10},{10,12},{12... | collective-permute-start | bytes 12296 | tf_op jit(solution)/shard_map/ppermute | solution.py:141
  186.2 3.6 %collective-permute-done.5 = f32[8,128]{1,0:T(8,128)S(1)} collective-permute-done((f32[8,128]{1,0:T(8,128)S(1)}, f32[8,128]{1,0:T(8,128)S(1)}, u32[]{:S(2)}, u32[]{:S(2)}) %collective-permute-start.5) | collective-permute-done | bytes 4128 | tf_op jit(solution)/shard_map/ppermute | solution.py:141
  189.8 2.2 %collective-permute-start.6 = (f32[8,128]{1,0:T(8,128)S(1)}, f32[8,128]{1,0:T(8,128)S(1)}, u32[]{:S(2)}, u32[]{:S(2)}) collective-permute-start(f32[8,128]{1,0:T(8,128)S(1)} %add.47), channel_id=1, source_target_pairs={{0,4},{2,6},{4,0},{6,2},{1,5},{3,7},{5,1},{7,3},{8,12},{10,14},{12... | collective-permute-start | bytes 12296 | tf_op jit(solution)/shard_map/ppermute | solution.py:141
  192.1 0.0 copy-done.5
  192.1 0.0 copy-done.6
  192.1 0.2 shard_map.84
  192.3 3.7 %collective-permute-done.6 = f32[8,128]{1,0:T(8,128)S(1)} collective-permute-done((f32[8,128]{1,0:T(8,128)S(1)}, f32[8,128]{1,0:T(8,128)S(1)}, u32[]{:S(2)}, u32[]{:S(2)}) %collective-permute-start.6) | collective-permute-done | bytes 4128 | tf_op jit(solution)/shard_map/ppermute | solution.py:141
  196.0 0.6 convert_bitcast_fusion
  196.6 0.5 all-to-all-done.1
  197.1 0.1 reshape.45.returned_ref
  197.3 0.8 shard_map.85
  (4 shorter events, 0.0 us)
Async XLA Ops:
  0.7 0.8 copy-start.3
  1.5 0.7 copy-start.4
  77.2 33.5 %copy-start.2 = (bf16[1,1536,384]{2,1,0:T(8,128)(2,1)S(1)}, bf16[1,1536,384]{2,1,0:T(8,128)(2,1)}, u32[]{:S(2)}) copy-start(bf16[1,1536,384]{2,1,0:T(8,128)(2,1)} %down_ref.7) | copy-start | bytes 3538948
  77.6 33.0 %copy-start = (bf16[1,1536,384]{2,1,0:T(8,128)(2,1)S(1)}, bf16[1,1536,384]{2,1,0:T(8,128)(2,1)}, u32[]{:S(2)}) copy-start(bf16[1,1536,384]{2,1,0:T(8,128)(2,1)} %gate_ref.7) | copy-start | bytes 3538948
  77.6 33.0 %copy-start.1 = (bf16[1,1536,384]{2,1,0:T(8,128)(2,1)S(1)}, bf16[1,1536,384]{2,1,0:T(8,128)(2,1)}, u32[]{:S(2)}) copy-start(bf16[1,1536,384]{2,1,0:T(8,128)(2,1)} %up_ref.7) | copy-start | bytes 3538948
  111.6 13.8 %collective-permute-start = (bf16[128,1536]{1,0:T(8,128)(2,1)S(1)}, bf16[128,1536]{1,0:T(8,128)(2,1)S(1)}, u32[]{:S(2)}, u32[]{:S(2)}) collective-permute-start(bf16[128,1536]{1,0:T(8,128)(2,1)S(1)} %shard_map.80), channel_id=1, source_target_pairs={{0,4},{2,6},{4,0},{6,2},{1,5},{3,7},{5,1},{7,3},{8,12},{10,14},{12... | collective-permute-start | bytes 1179656 | tf_op jit(solution)/shard_map/ppermute | solution.py:141
  116.1 18.4 %collective-permute-start.1 = (bf16[128,1536]{1,0:T(8,128)(2,1)S(1)}, bf16[128,1536]{1,0:T(8,128)(2,1)S(1)}, u32[]{:S(2)}, u32[]{:S(2)}) collective-permute-start(bf16[128,1536]{1,0:T(8,128)(2,1)S(1)} %shard_map.81), channel_id=1, source_target_pairs={{0,2},{2,4},{4,6},{6,0},{1,3},{3,5},{5,7},{7,1},{8,10},{10,12},{12... | collective-permute-start | bytes 1179656 | tf_op jit(solution)/shard_map/ppermute | solution.py:141
  119.1 15.5 %collective-permute-start.2 = (bf16[128,1536]{1,0:T(8,128)(2,1)S(1)}, bf16[128,1536]{1,0:T(8,128)(2,1)S(1)}, u32[]{:S(2)}, u32[]{:S(2)}) collective-permute-start(bf16[128,1536]{1,0:T(8,128)(2,1)S(1)} %shard_map.82), channel_id=1, source_target_pairs={{0,6},{2,0},{4,2},{6,4},{1,7},{3,1},{5,3},{7,5},{8,14},{10,8},{12,... | collective-permute-start | bytes 1179656 | tf_op jit(solution)/shard_map/ppermute | solution.py:141
  134.7 57.3 %copy-start.5 = (s32[16,4]{0,1:T(4,128)S(1)}, s32[16,4]{0,1:T(4,128)}, u32[]{:S(2)}) copy-start(s32[16,4]{0,1:T(4,128)} %param.7) | copy-start | bytes 772
  134.7 57.3 %copy-start.6 = (f32[16,4]{0,1:T(4,128)S(1)}, f32[16,4]{0,1:T(4,128)}, u32[]{:S(2)}) copy-start(f32[16,4]{0,1:T(4,128)} %param.8) | copy-start | bytes 772
  135.9 61.2 %all-to-all-start.1 = ((bf16[64,2,1536]{2,1,0:T(2,128)(2,1)}), bf16[64,2,1536]{2,1,0:T(2,128)(2,1)S(1)}, u32[]{:S(2)}, u32[]{:S(2)}) async-start(bf16[64,2,1536]{2,1,0:T(2,128)(2,1)} %bitcast.9), calls=%async_computation.1 | async-start | bytes 786432 | tf_op jit(solution)/shard_map/all_to_all | solution.py:136
  150.3 29.9 %collective-permute-start.3 = (f32[8,128]{1,0:T(8,128)S(1)}, f32[8,128]{1,0:T(8,128)S(1)}, u32[]{:S(2)}, u32[]{:S(2)}) collective-permute-start(f32[8,128]{1,0:T(8,128)S(1)} %get-tuple-element.21), channel_id=1, source_target_pairs={{0,8},{8,0},{1,9},{9,1},{2,10},{10,2},{3,11},{11,3},{4,12},{12,4},... | collective-permute-start | bytes 12296 | tf_op jit(solution)/shard_map/ppermute | solution.py:141
  180.2 3.8 %collective-permute-start.4 = (f32[8,128]{1,0:T(8,128)S(1)}, f32[8,128]{1,0:T(8,128)S(1)}, u32[]{:S(2)}, u32[]{:S(2)}) collective-permute-start(f32[8,128]{1,0:T(8,128)S(1)} %add.45), channel_id=1, source_target_pairs={{0,1},{1,0},{2,3},{3,2},{4,5},{5,4},{6,7},{7,6},{8,9},{9,8},{10,11... | collective-permute-start | bytes 12296 | tf_op jit(solution)/shard_map/ppermute | solution.py:141
  184.0 5.9 %collective-permute-start.5 = (f32[8,128]{1,0:T(8,128)S(1)}, f32[8,128]{1,0:T(8,128)S(1)}, u32[]{:S(2)}, u32[]{:S(2)}) collective-permute-start(f32[8,128]{1,0:T(8,128)S(1)} %add.46), channel_id=1, source_target_pairs={{0,2},{2,4},{4,6},{6,0},{1,3},{3,5},{5,7},{7,1},{8,10},{10,12},{12... | collective-permute-start | bytes 12296 | tf_op jit(solution)/shard_map/ppermute | solution.py:141
  189.8 6.2 %collective-permute-start.6 = (f32[8,128]{1,0:T(8,128)S(1)}, f32[8,128]{1,0:T(8,128)S(1)}, u32[]{:S(2)}, u32[]{:S(2)}) collective-permute-start(f32[8,128]{1,0:T(8,128)S(1)} %add.47), channel_id=1, source_target_pairs={{0,4},{2,6},{4,0},{6,2},{1,5},{3,7},{5,1},{7,3},{8,12},{10,14},{12... | collective-permute-start | bytes 12296 | tf_op jit(solution)/shard_map/ppermute | solution.py:141

commit v7 on v6

--- a/solution.py
+++ b/solution.py
@@ -1,3 +1,5 @@
+import functools
+
 import jax
 import jax.numpy as jnp
 from jax import lax
@@ -8,8 +10,6 @@
 
 NEAR = 2
 SLOTS = 2
-CORES = 2
-BLOCK = NEAR * CORES
 SUBLANES = 8
 
 f32, bf16 = jnp.float32, jnp.bfloat16
@@ -50,29 +50,29 @@
     out_ref[:, width:] = placed(ids_ref[...], lanes, lane % half, lane // half).astype(bf16)
 
 
-def gates_kernel(ids_ref, weights_ref, high_ref, low_ref):
+def gates_kernel(dp, ids_ref, weights_ref, high_ref, low_ref):
     lanes = high_ref.shape[1]
     lane = iota(high_ref.shape, 1)
     half = lanes // SLOTS
     slot = lane // SLOTS
-    chip = slot % (half // CORES)
-    expert = chip // NEAR * BLOCK + chip % NEAR * CORES + slot // (half // CORES)
+    chip = slot % (half // dp)
+    expert = chip // NEAR * (NEAR * dp) + chip % NEAR * dp + slot // (half // dp)
     mix = placed(ids_ref[...], lanes, expert, lane % SLOTS, weights_ref[...])
     high = mix.astype(bf16)
     high_ref[...] = high
     low_ref[...] = (mix - high.astype(f32)).astype(bf16)
 
 
-def select_kernel(block_ref, gathered_ref, out_ref, loads_ref):
+def select_kernel(dp, block_ref, gathered_ref, out_ref, loads_ref):
     copies, count, width = out_ref.shape
     lanes = gathered_ref.shape[1] - width
     tokens = gathered_ref.shape[0]
     experts = lanes // SLOTS
-    far = count // (SLOTS * BLOCK)
+    far = count // (SLOTS * NEAR * dp)
     row = iota((lanes, count), 1)
     lane = iota((lanes, count), 0)
     device = row // (far * SLOTS)
-    expert = block_ref[0] * BLOCK + device % NEAR * CORES + device // NEAR
+    expert = block_ref[0] * (NEAR * dp) + device % NEAR * dp + device // NEAR
     pick = jnp.where(lane == row % SLOTS * experts + expert, 1.0, 0.0).astype(bf16)
     chosen = jnp.dot(gathered_ref[:, width:], pick, preferred_element_type=f32)
     source = iota((tokens, count), 0) // (tokens // far)
@@ -161,7 +161,7 @@
     packed, block, *peers = lax.optimization_barrier((packed, block, *peers))
     gathered = lax.all_gather(packed, "eh", tiled=True)
     outgoing, loads = pl.pallas_call(
-        select_kernel,
+        functools.partial(select_kernel, dp),
         out_shape=(
             jax.ShapeDtypeStruct((tp, slots, width), bf16),
             jax.ShapeDtypeStruct((SUBLANES, slots), f32),
@@ -196,7 +196,7 @@
             loads = loads + other
             step, turn = 2 * step, turn + 1
     high, low = pl.pallas_call(
-        gates_kernel,
+        functools.partial(gates_kernel, dp),
         out_shape=(jax.ShapeDtypeStruct((count, slots), bf16),) * 2,
         in_specs=[WHOLE] * 2,
         out_specs=(WHOLE, WHOLE),

time: 199 us -> 199 us (level)
  no operation moved by 1% of the time
where the time goes in v7:
time: 199 us; the launch traced here: 198 us
  blocking collectives  108 us (54%)
  waiting for transfers between devices  45.1 us (23%)
  starting transfers between devices  35.1 us (18%)
  Pallas kernels  5.9 us (3%)
  local copies, waits for them, and re-layouts  2.82 us (1%)
    all_gather x1, blocking collectives, per_device(): gathered = lax.all_gather(packed, 'eh', tiled=True)  74.8 us
    ppermute x7, waiting for transfers between devices, shifted(): lax.ppermute(array, axis, [(i, (i + step) % size) for i in range(size)])  44.6 us
    all_to_all x1, blocking collectives, all_to_all(): return lax.all_to_all(array, axis, split_axis=0, concat_axis=0, tiled=True)  33 us
    ppermute x7, starting transfers between devices, shifted(): lax.ppermute(array, axis, [(i, (i + step) % size) for i in range(size)])  20.7 us
    all_to_all x1, starting transfers between devices, all_to_all(): return lax.all_to_all(array, axis, split_axis=0, concat_axis=0, tiled=True)  14.3 us
  transfers between devices with their start and end apart: 8, of which 7 were waited for; matrix products, arithmetic and copies ran while one was open for 0% of the time, Pallas kernels for 2%

profile of v7, /device:TPU:33, one launch (start us, length us, event | category | flops | bytes accessed | tf_op | source)
XLA Modules:
  0.0 198.1 jit_solution(13017991599210543154)
XLA Ops:
  0.7 0.0 copy-start.3
  0.7 0.8 copy-done.3
  1.5 0.0 copy-start.4
  1.5 0.7 copy-done.4
  2.2 0.2 shard_map.77
  2.4 74.8 %all_gather.3.gathered_ref = bf16[256,1664]{1,0:T(8,128)(2,1)S(1)} all-gather(bf16[16,1664]{1,0:T(8,128)(2,1)S(1)} %shard_map.77), channel_id=1, replica_groups=mesh['groups'=2,'eh'=16,'el'=2,'tp'=4,'dp'=2] {'eh'}, dimensions={0}, use_global_device_ids=true | all-gather | bytes 905216 | tf_op jit(solution)/shard_map/all_gather | solution.py:162
  77.2 0.0 copy-start.2
  77.2 0.5 shard_map.78
  77.6 0.0 copy-start
  77.6 0.0 copy-start.1
  77.7 33.0 %all_to_all.10 = bf16[16,32,1536]{2,1,0:T(8,128)(2,1)S(1)} all-to-all(bf16[16,32,1536]{2,1,0:T(8,128)(2,1)S(1)} %bitcast.17), channel_id=1, replica_groups=mesh['groups'=2,'eh'=16,'el'=2,'tp'=4,'dp'=2] {'tp','dp','el'}, dimensions={0} | all-to-all | bytes 3145728 | tf_op jit(solution)/shard_map/all_to_all | solution.py:136
  110.6 0.0 copy-done.2
  110.6 0.0 copy-done
  110.6 0.0 copy-done.1
  110.6 1.0 shard_map.80
  111.6 3.5 %collective-permute-start = (bf16[128,1536]{1,0:T(8,128)(2,1)S(1)}, bf16[128,1536]{1,0:T(8,128)(2,1)S(1)}, u32[]{:S(2)}, u32[]{:S(2)}) collective-permute-start(bf16[128,1536]{1,0:T(8,128)(2,1)S(1)} %shard_map.80), channel_id=1, source_target_pairs={{0,4},{2,6},{4,0},{6,2},{1,5},{3,7},{5,1},{7,3},{8,12},{10,14},{12... | collective-permute-start | bytes 1179656 | tf_op jit(solution)/shard_map/ppermute | solution.py:141
  115.1 1.0 shard_map.81
  116.1 2.0 collective-permute-start.1
  118.1 1.0 shard_map.82
  119.1 4.6 %collective-permute-start.2 = (bf16[128,1536]{1,0:T(8,128)(2,1)S(1)}, bf16[128,1536]{1,0:T(8,128)(2,1)S(1)}, u32[]{:S(2)}, u32[]{:S(2)}) collective-permute-start(bf16[128,1536]{1,0:T(8,128)(2,1)S(1)} %shard_map.82), channel_id=1, source_target_pairs={{0,6},{2,0},{4,2},{6,4},{1,7},{3,1},{5,3},{7,5},{8,14},{10,8},{12,... | collective-permute-start | bytes 1179656 | tf_op jit(solution)/shard_map/ppermute | solution.py:141
  123.7 1.0 shard_map.79.own_ref
  124.7 0.8 collective-permute-done.refs_0_
  125.4 9.1 %collective-permute-done.1.refs_1_ = bf16[128,1536]{1,0:T(8,128)(2,1)S(1)} collective-permute-done((bf16[128,1536]{1,0:T(8,128)(2,1)S(1)}, bf16[128,1536]{1,0:T(8,128)(2,1)S(1)}, u32[]{:S(2)}, u32[]{:S(2)}) %collective-permute-start.1) | collective-permute-done | bytes 393248 | tf_op jit(solution)/shard_map/ppermute | solution.py:141
  134.5 0.0 collective-permute-done.2.refs_2_
  134.5 0.2 shard_map.83
  134.7 0.0 copy-start.5
  134.7 0.0 copy-start.6
  134.8 0.1 reshape.43
  134.9 1.0 copy.8
  135.9 14.3 %all-to-all-start.1 = ((bf16[64,2,1536]{2,1,0:T(2,128)(2,1)}), bf16[64,2,1536]{2,1,0:T(2,128)(2,1)S(1)}, u32[]{:S(2)}, u32[]{:S(2)}) async-start(bf16[64,2,1536]{2,1,0:T(2,128)(2,1)} %bitcast.9), calls=%async_computation.1 | async-start | bytes 786432 | tf_op jit(solution)/shard_map/all_to_all | solution.py:136
  150.3 3.3 %collective-permute-start.3 = (f32[8,128]{1,0:T(8,128)S(1)}, f32[8,128]{1,0:T(8,128)S(1)}, u32[]{:S(2)}, u32[]{:S(2)}) collective-permute-start(f32[8,128]{1,0:T(8,128)S(1)} %get-tuple-element.21), channel_id=1, source_target_pairs={{0,8},{8,0},{1,9},{9,1},{2,10},{10,2},{3,11},{11,3},{4,12},{12,4},... | collective-permute-start | bytes 12296 | tf_op jit(solution)/shard_map/ppermute | solution.py:141
  153.6 26.6 %collective-permute-done.3 = f32[8,128]{1,0:T(8,128)S(1)} collective-permute-done((f32[8,128]{1,0:T(8,128)S(1)}, f32[8,128]{1,0:T(8,128)S(1)}, u32[]{:S(2)}, u32[]{:S(2)}) %collective-permute-start.3) | collective-permute-done | bytes 4128 | tf_op jit(solution)/shard_map/ppermute | solution.py:141
  180.2 2.9 %collective-permute-start.4 = (f32[8,128]{1,0:T(8,128)S(1)}, f32[8,128]{1,0:T(8,128)S(1)}, u32[]{:S(2)}, u32[]{:S(2)}) collective-permute-start(f32[8,128]{1,0:T(8,128)S(1)} %add.45), channel_id=1, source_target_pairs={{0,1},{1,0},{2,3},{3,2},{4,5},{5,4},{6,7},{7,6},{8,9},{9,8},{10,11... | collective-permute-start | bytes 12296 | tf_op jit(solution)/shard_map/ppermute | solution.py:141
  183.2 0.8 collective-permute-done.4
  184.0 2.2 %collective-permute-start.5 = (f32[8,128]{1,0:T(8,128)S(1)}, f32[8,128]{1,0:T(8,128)S(1)}, u32[]{:S(2)}, u32[]{:S(2)}) collective-permute-start(f32[8,128]{1,0:T(8,128)S(1)} %add.46), channel_id=1, source_target_pairs={{0,2},{2,4},{4,6},{6,0},{1,3},{3,5},{5,7},{7,1},{8,10},{10,12},{12... | collective-permute-start | bytes 12296 | tf_op jit(solution)/shard_map/ppermute | solution.py:141
  186.2 3.6 %collective-permute-done.5 = f32[8,128]{1,0:T(8,128)S(1)} collective-permute-done((f32[8,128]{1,0:T(8,128)S(1)}, f32[8,128]{1,0:T(8,128)S(1)}, u32[]{:S(2)}, u32[]{:S(2)}) %collective-permute-start.5) | collective-permute-done | bytes 4128 | tf_op jit(solution)/shard_map/ppermute | solution.py:141
  189.8 2.2 %collective-permute-start.6 = (f32[8,128]{1,0:T(8,128)S(1)}, f32[8,128]{1,0:T(8,128)S(1)}, u32[]{:S(2)}, u32[]{:S(2)}) collective-permute-start(f32[8,128]{1,0:T(8,128)S(1)} %add.47), channel_id=1, source_target_pairs={{0,4},{2,6},{4,0},{6,2},{1,5},{3,7},{5,1},{7,3},{8,12},{10,14},{12... | collective-permute-start | bytes 12296 | tf_op jit(solution)/shard_map/ppermute | solution.py:141
  192.1 0.0 copy-done.5
  192.1 0.0 copy-done.6
  192.1 0.2 shard_map.84
  192.3 3.7 %collective-permute-done.6 = f32[8,128]{1,0:T(8,128)S(1)} collective-permute-done((f32[8,128]{1,0:T(8,128)S(1)}, f32[8,128]{1,0:T(8,128)S(1)}, u32[]{:S(2)}, u32[]{:S(2)}) %collective-permute-start.6) | collective-permute-done | bytes 4128 | tf_op jit(solution)/shard_map/ppermute | solution.py:141
  196.0 0.6 convert_bitcast_fusion
  196.6 0.5 all-to-all-done.1
  197.1 0.1 reshape.45.returned_ref
  197.3 0.8 shard_map.85
  (4 shorter events, 0.0 us)
Async XLA Ops:
  0.7 0.8 copy-start.3
  1.5 0.7 copy-start.4
  77.2 33.5 %copy-start.2 = (bf16[1,1536,384]{2,1,0:T(8,128)(2,1)S(1)}, bf16[1,1536,384]{2,1,0:T(8,128)(2,1)}, u32[]{:S(2)}) copy-start(bf16[1,1536,384]{2,1,0:T(8,128)(2,1)} %down_ref.7) | copy-start | bytes 3538948
  77.6 33.0 %copy-start = (bf16[1,1536,384]{2,1,0:T(8,128)(2,1)S(1)}, bf16[1,1536,384]{2,1,0:T(8,128)(2,1)}, u32[]{:S(2)}) copy-start(bf16[1,1536,384]{2,1,0:T(8,128)(2,1)} %gate_ref.7) | copy-start | bytes 3538948
  77.6 33.0 %copy-start.1 = (bf16[1,1536,384]{2,1,0:T(8,128)(2,1)S(1)}, bf16[1,1536,384]{2,1,0:T(8,128)(2,1)}, u32[]{:S(2)}) copy-start(bf16[1,1536,384]{2,1,0:T(8,128)(2,1)} %up_ref.7) | copy-start | bytes 3538948
  111.6 13.8 %collective-permute-start = (bf16[128,1536]{1,0:T(8,128)(2,1)S(1)}, bf16[128,1536]{1,0:T(8,128)(2,1)S(1)}, u32[]{:S(2)}, u32[]{:S(2)}) collective-permute-start(bf16[128,1536]{1,0:T(8,128)(2,1)S(1)} %shard_map.80), channel_id=1, source_target_pairs={{0,4},{2,6},{4,0},{6,2},{1,5},{3,7},{5,1},{7,3},{8,12},{10,14},{12... | collective-permute-start | bytes 1179656 | tf_op jit(solution)/shard_map/ppermute | solution.py:141
  116.1 18.4 %collective-permute-start.1 = (bf16[128,1536]{1,0:T(8,128)(2,1)S(1)}, bf16[128,1536]{1,0:T(8,128)(2,1)S(1)}, u32[]{:S(2)}, u32[]{:S(2)}) collective-permute-start(bf16[128,1536]{1,0:T(8,128)(2,1)S(1)} %shard_map.81), channel_id=1, source_target_pairs={{0,2},{2,4},{4,6},{6,0},{1,3},{3,5},{5,7},{7,1},{8,10},{10,12},{12... | collective-permute-start | bytes 1179656 | tf_op jit(solution)/shard_map/ppermute | solution.py:141
  119.1 15.5 %collective-permute-start.2 = (bf16[128,1536]{1,0:T(8,128)(2,1)S(1)}, bf16[128,1536]{1,0:T(8,128)(2,1)S(1)}, u32[]{:S(2)}, u32[]{:S(2)}) collective-permute-start(bf16[128,1536]{1,0:T(8,128)(2,1)S(1)} %shard_map.82), channel_id=1, source_target_pairs={{0,6},{2,0},{4,2},{6,4},{1,7},{3,1},{5,3},{7,5},{8,14},{10,8},{12,... | collective-permute-start | bytes 1179656 | tf_op jit(solution)/shard_map/ppermute | solution.py:141
  134.7 57.3 %copy-start.5 = (s32[16,4]{0,1:T(4,128)S(1)}, s32[16,4]{0,1:T(4,128)}, u32[]{:S(2)}) copy-start(s32[16,4]{0,1:T(4,128)} %param.7) | copy-start | bytes 772
  134.7 57.3 %copy-start.6 = (f32[16,4]{0,1:T(4,128)S(1)}, f32[16,4]{0,1:T(4,128)}, u32[]{:S(2)}) copy-start(f32[16,4]{0,1:T(4,128)} %param.8) | copy-start | bytes 772
  135.9 61.2 %all-to-all-start.1 = ((bf16[64,2,1536]{2,1,0:T(2,128)(2,1)}), bf16[64,2,1536]{2,1,0:T(2,128)(2,1)S(1)}, u32[]{:S(2)}, u32[]{:S(2)}) async-start(bf16[64,2,1536]{2,1,0:T(2,128)(2,1)} %bitcast.9), calls=%async_computation.1 | async-start | bytes 786432 | tf_op jit(solution)/shard_map/all_to_all | solution.py:136
  150.3 29.9 %collective-permute-start.3 = (f32[8,128]{1,0:T(8,128)S(1)}, f32[8,128]{1,0:T(8,128)S(1)}, u32[]{:S(2)}, u32[]{:S(2)}) collective-permute-start(f32[8,128]{1,0:T(8,128)S(1)} %get-tuple-element.21), channel_id=1, source_target_pairs={{0,8},{8,0},{1,9},{9,1},{2,10},{10,2},{3,11},{11,3},{4,12},{12,4},... | collective-permute-start | bytes 12296 | tf_op jit(solution)/shard_map/ppermute | solution.py:141
  180.2 3.8 %collective-permute-start.4 = (f32[8,128]{1,0:T(8,128)S(1)}, f32[8,128]{1,0:T(8,128)S(1)}, u32[]{:S(2)}, u32[]{:S(2)}) collective-permute-start(f32[8,128]{1,0:T(8,128)S(1)} %add.45), channel_id=1, source_target_pairs={{0,1},{1,0},{2,3},{3,2},{4,5},{5,4},{6,7},{7,6},{8,9},{9,8},{10,11... | collective-permute-start | bytes 12296 | tf_op jit(solution)/shard_map/ppermute | solution.py:141
  184.0 5.9 %collective-permute-start.5 = (f32[8,128]{1,0:T(8,128)S(1)}, f32[8,128]{1,0:T(8,128)S(1)}, u32[]{:S(2)}, u32[]{:S(2)}) collective-permute-start(f32[8,128]{1,0:T(8,128)S(1)} %add.46), channel_id=1, source_target_pairs={{0,2},{2,4},{4,6},{6,0},{1,3},{3,5},{5,7},{7,1},{8,10},{10,12},{12... | collective-permute-start | bytes 12296 | tf_op jit(solution)/shard_map/ppermute | solution.py:141
  189.8 6.2 %collective-permute-start.6 = (f32[8,128]{1,0:T(8,128)S(1)}, f32[8,128]{1,0:T(8,128)S(1)}, u32[]{:S(2)}, u32[]{:S(2)}) collective-permute-start(f32[8,128]{1,0:T(8,128)S(1)} %add.47), channel_id=1, source_target_pairs={{0,4},{2,6},{4,0},{6,2},{1,5},{3,7},{5,1},{7,3},{8,12},{10,14},{12... | collective-permute-start | bytes 12296 | tf_op jit(solution)/shard_map/ppermute | solution.py:141
